TPU v7x, 32 devices: a whole 2x2x4 slice. The times are simulated.
32 devices in a mesh: gx: 2 (over x), gy: 4 (over y, core), gz: 4 (over z).
Axes of the slice: x: 2, y: 2, z: 4, core: 2. Of those that a mesh axis runs over, the one named last changes fastest.
Arguments:
- velocity: float32 [3, 32, 128, 512], P(None, 'gx', 'gy', 'gz'), may hold values from -6 to 6
- forcing: float32 [3, 32, 128, 512], P(None, 'gx', 'gy', 'gz'), may hold values from -12 to 12
- phase_block: int32 [8, 32, 128], P('gx', 'gy', 'gz'), may hold values from 0 to 7
- prefactor: float32 [8], replicated, may hold values from 0.5 to 4
- yield_stress: float32 [8], replicated, may hold values from 1 to 16
Outputs:
- smoothed: float32 [3, 32, 128, 512], P(None, 'gx', 'gy', 'gz')
- viscosity_field: float32 [32, 128, 512], P('gx', 'gy', 'gz')
- coarse_one: float32 [16, 64, 256], P('gx', 'gy', 'gz')
- coarse_two: float32 [8, 32, 128], P('gx', 'gy', 'gz')
- coarse_three: float32 [4, 16, 64], P('gx', 'gy', 'gz')
- residual_field: float32 [3, 32, 128, 512], P(None, 'gx', 'gy', 'gz')
- residual_rms: float32 [], replicated
All inputs are finite; a program needn't handle non-finite values.
Results may differ from a plain program's by a relative error of at most 0.000053.
Values sent between devices are 32-bit elements; how exact they have to be, the bound alone decides.
A program may use at most 64 MiB of HBM per device.

v0:
```python
import functools

import jax
import jax.numpy as jnp
import numpy as np
from jax import lax
from jax.experimental import pallas as pl
from jax.experimental.pallas import tpu as pltpu
from jax.sharding import PartitionSpec as P

BLOCK = 4
RELAXATION = 0.8
PAD = 8
GHOST = 64
UNROLL = 2
ONE_STAGE = 32
MESH = pl.DeviceIdType.MESH
HIGHEST = lax.Precision.HIGHEST


def coarse_matrices(length):
    def chain(low_edge, high_edge):
        field = np.eye(length)
        found = []
        first = 0
        for _ in range(3):
            count = length >> (len(found) + 1)
            out = np.zeros((length, count + 2))
            for k in range(-1, count + 1):
                for shift, weight in ((-1, 1.0), (0, 3.0), (1, 3.0), (2, 1.0)):
                    source = 2 * k + shift - first
                    if 0 <= source < field.shape[1]:
                        out[:, k + 1] += weight / 8.0 * field[:, source]
            if low_edge:
                out[:, 0] = 0.0
            if high_edge:
                out[:, -1] = 0.0
            placed = np.zeros((length, length))
            placed[:, :count] = out[:, 1:-1]
            placed[:, GHOST] = out[:, 0]
            placed[:, GHOST + 1] = out[:, -1]
            found.append(placed)
            field = out
            first = -1
        return np.stack(found)

    inner = chain(False, False)
    return np.stack([inner, inner - chain(True, False), inner - chain(False, True)]).astype(np.float32)


def kernel(
    sizes,
    vel_hbm,
    forc_hbm,
    mats_hbm,
    phase_hbm,
    pref_hbm,
    yield_hbm,
    smooth_ref,
    visc_ref,
    one_ref,
    two_ref,
    three_ref,
    misfit_ref,
    rms_ref,
    v0,
    v1,
    v2,
    visc,
    forc,
    mats,
    phase_ref,
    pref_ref,
    yield_ref,
    faces,
    z_faces,
    early,
    weight,
    diag,
    pref_cells,
    yield_cells,
    y_send,
    y_recv,
    z_send,
    z_recv,
    cx1,
    cx2,
    cx3,
    gx_send,
    gx_recv,
    t1,
    t2a,
    t2b,
    t3a,
    t3b,
    t3c,
    gy_send,
    gy_recv,
    gz_send,
    gz_recv,
    sums_xy,
    sums_z,
    local_sem,
    send_sem,
    recv_sem,
    plane_send,
    plane_recv,
    line_send,
    line_recv,
):
    nx, ny, nz, cx, cy, cz, phases = sizes
    ix, iy, iz = lax.axis_index("gx"), lax.axis_index("gy"), lax.axis_index("gz")
    rows = pl.ds(PAD, cy)

    vel_in = pltpu.make_async_copy(vel_hbm, v0.at[:, pl.ds(1, cx), rows, :], local_sem.at[0])
    forc_in = pltpu.make_async_copy(forc_hbm, forc, local_sem.at[1])
    mats_in = pltpu.make_async_copy(mats_hbm, mats, local_sem.at[2])
    vel_in.start()
    forc_in.start()
    mats_in.start()
    phase_in = pltpu.make_async_copy(phase_hbm, phase_ref, local_sem.at[3])
    phase_in.start()
    pref_in = pltpu.make_async_copy(pref_hbm, pref_ref, local_sem.at[4])
    pref_in.start()
    yield_in = pltpu.make_async_copy(yield_hbm, yield_ref, local_sem.at[5])
    yield_in.start()

    plane0 = jnp.zeros((3, cy, cz), jnp.float32)
    for buf in (v0, v1, v2):
        buf[:, 0, rows, :] = plane0
        buf[:, cx + 1, rows, :] = plane0
    row0 = jnp.zeros((3, cx, 1, cz), jnp.float32)
    visc[1 : cx + 1, PAD - 1 : PAD, :] = row0[0]
    visc[1 : cx + 1, PAD + cy : PAD + cy + 1, :] = row0[0]
    for buf in (v1, v2):
        buf[:, 1 : cx + 1, PAD - 1 : PAD, :] = row0
        buf[:, 1 : cx + 1, PAD + cy : PAD + cy + 1, :] = row0
    visc[0, rows, :] = plane0[0]
    visc[cx + 1, rows, :] = plane0[0]
    y_recv[...] = jnp.zeros(y_recv.shape, jnp.float32)
    z_recv[...] = jnp.zeros(z_recv.shape, jnp.float32)
    gx_recv[...] = jnp.zeros(gx_recv.shape, jnp.float32)
    gy_recv[...] = jnp.zeros(gy_recv.shape, jnp.float32)
    gz_recv[...] = jnp.zeros(gz_recv.shape, jnp.float32)

    barrier = pltpu.get_barrier_semaphore()
    me_xy = ix * ny + iy
    one_stage = nx * ny * nz <= ONE_STAGE
    plane_peers = []
    if one_stage:
        me_first = me_xy * nz + iz
        for k in range(1, nx * ny * nz):
            other = lax.rem(me_first + k, nx * ny * nz)
            plane_peers.append((other // (ny * nz), lax.rem(other // nz, ny), lax.rem(other, nz)))
        line_peers = []
    else:
        me_first = me_xy
        for k in range(1, nx * ny):
            other = lax.rem(me_xy + k, nx * ny)
            plane_peers.append((other // ny, lax.rem(other, ny), iz))
        line_peers = [(ix, iy, lax.rem(iz + k, nz)) for k in range(1, nz)]
    for peer in plane_peers + line_peers:
        pl.semaphore_signal(barrier, inc=1, device_id=peer, device_id_type=MESH)

    lane = lax.broadcasted_iota(jnp.int32, (cy, cz), 1)
    odd_lane = lax.rem(lane, 2) == 1
    first_lane = lane == 0
    last_lane = lane == cz - 1

    up_ids = (
        (lax.rem(ix + 1, nx), iy, iz),
        (ix, lax.rem(iy + 1, ny), iz),
        (ix, iy, lax.rem(iz + 1, nz)),
    )
    down_ids = (
        (lax.rem(ix + nx - 1, nx), iy, iz),
        (ix, lax.rem(iy + ny - 1, ny), iz),
        (ix, iy, lax.rem(iz + nz - 1, nz)),
    )
    has_up = (ix < nx - 1, iy < ny - 1, iz < nz - 1)
    has_down = (ix > 0, iy > 0, iz > 0)
    started = []

    def exchange(slot, dim, up_src, up_dst, down_src, down_dst):
        up = pltpu.make_async_remote_copy(
            up_src, up_dst, send_sem.at[slot, 0], recv_sem.at[slot, 0],
            device_id=up_ids[dim], device_id_type=MESH,
        )
        down = pltpu.make_async_remote_copy(
            down_src, down_dst, send_sem.at[slot, 1], recv_sem.at[slot, 1],
            device_id=down_ids[dim], device_id_type=MESH,
        )
        pl.when(has_up[dim])(up.start)
        pl.when(has_down[dim])(down.start)
        started.append((has_up[dim], up))
        started.append((has_down[dim], down))

        def wait():
            pl.when(has_down[dim])(up.wait_recv)
            pl.when(has_up[dim])(down.wait_recv)

        return wait

    def send_x(r, buf, vector):
        if vector:
            return exchange(
                3 * r, 0,
                buf.at[:, cx, rows, :], buf.at[:, 0, rows, :],
                buf.at[:, 1, rows, :], buf.at[:, cx + 1, rows, :],
            )
        return exchange(
            3 * r, 0,
            buf.at[cx, rows, :], buf.at[0, rows, :],
            buf.at[1, rows, :], buf.at[cx + 1, rows, :],
        )

    def send_yz(r):
        held = pl.ds(0, 1 if r == 1 else 3)
        return [
            exchange(
                3 * r + 1, 1,
                y_send.at[r, 0, held], y_recv.at[r, 0, held],
                y_send.at[r, 1, held], y_recv.at[r, 1, held],
            ),
            exchange(3 * r + 2, 2, z_send.at[r], z_recv.at[r, 0], z_send.at[r], z_recv.at[r, 1]),
        ]

    def pack(r, comp, i, value, packed):
        y_send[r, 0, comp, pl.ds(i, 1), :] = value[cy - 1 : cy, :]
        y_send[r, 1, comp, pl.ds(i, 1), :] = value[0:1, :]
        place = 2 * (comp * cx + i) + 1
        here = (lane == place) | (lane == place + 1)
        return jnp.where(here, pltpu.roll(value, place + 1, 1), packed)

    def unpack_y(r, buf, comps):
        def body(i, carry):
            for comp in range(comps):
                target = buf.at[comp, i + 1] if comps == 3 else buf.at[i + 1]
                target[PAD - 1 : PAD, :] = y_recv[r, 0, comp, pl.ds(i, 1), :]
                target[PAD + cy : PAD + cy + 1, :] = y_recv[r, 1, comp, pl.ds(i, 1), :]
            return carry

        lax.fori_loop(0, cx, body, 0)

    def merged_z(r):
        return jnp.where(odd_lane, z_recv[r, 0], pltpu.roll(z_recv[r, 1], cz - 2, 1))

    def along(plane_ref, centre, merged, place):
        edge = pltpu.roll(merged, cz - 1 - 2 * place, 1)
        return (
            plane_ref[PAD - 1 : PAD - 1 + cy, :],
            plane_ref[PAD + 1 : PAD + 1 + cy, :],
            jnp.where(first_lane, edge, pltpu.roll(centre, 1, 1)),
            jnp.where(last_lane, edge, pltpu.roll(centre, cz - 1, 1)),
        )

    def around(buf, comp, i, merged):
        centre = buf[comp, i + 1, rows, :]
        ym, yp, zm, zp = along(buf.at[comp, i + 1], centre, merged, comp * cx + i)
        return centre, (buf[comp, i, rows, :], buf[comp, i + 2, rows, :], ym, yp, zm, zp)

    vel_in.wait()

    def pack_first(i, packed):
        for comp in range(3):
            packed = pack(0, comp, i, v0[comp, i + 1, rows, :], packed)
        return packed

    nothing = jnp.zeros((cy, cz), jnp.float32)
    z_send[0] = lax.fori_loop(0, cx, pack_first, nothing, unroll=UNROLL)
    pl.semaphore_wait(barrier, len(plane_peers) + len(line_peers))
    waits = [send_x(0, v0, True)] + send_yz(0)

    phase_in.wait()
    pref_in.wait()
    yield_in.wait()
    blocks = phase_ref[...].astype(jnp.float32)
    n_rows, n_blocks = blocks.shape
    spread_z = lax.broadcasted_iota(jnp.int32, (n_blocks, cz), 1) // BLOCK
    spread_z = (spread_z == lax.broadcasted_iota(jnp.int32, (n_blocks, cz), 0)).astype(jnp.float32)
    spread_y = lax.broadcasted_iota(jnp.int32, (n_rows * BLOCK, n_rows), 0) // BLOCK
    spread_y = (
        spread_y == lax.broadcasted_iota(jnp.int32, (n_rows * BLOCK, n_rows), 1)
    ).astype(jnp.float32)
    cells = jnp.dot(blocks, spread_z, preferred_element_type=jnp.float32, precision=HIGHEST)
    cells = jnp.dot(spread_y, cells, preferred_element_type=jnp.float32, precision=HIGHEST)
    for bx in range(cx // BLOCK):
        phase = cells[bx * cy : (bx + 1) * cy, :]
        pref_value = jnp.zeros((cy, cz), jnp.float32)
        yield_value = jnp.zeros((cy, cz), jnp.float32)
        for p in range(phases):
            here = jnp.abs(phase - float(p)) < 0.5
            pref_value = jnp.where(here, pref_ref[p], pref_value)
            yield_value = jnp.where(here, yield_ref[p], yield_value)
        pref_cells[bx] = pref_value
        yield_cells[bx] = 0.5 * yield_value
    for buf in (cx1, cx2, cx3):
        for edge in (0, PAD + cy):
            buf[:, edge : edge + PAD, :] = jnp.zeros((buf.shape[0], PAD, cz), jnp.float32)
    for buf in (t1, t2a, t2b, t3a, t3b, t3c):
        buf[...] = jnp.zeros(buf.shape, jnp.float32)

    for wait in waits:
        wait()
    unpack_y(0, v0, 3)
    merged0 = merged_z(0)

    def ends_first(body, r, buf, vector, inner=None):
        packed = lax.fori_loop(0, 2, lambda t, carry: body(t * (cx - 1), carry), nothing)
        sent = send_x(r, buf, vector)
        z_send[r] = lax.fori_loop(1, cx - 1, inner or body, packed, unroll=UNROLL)
        return [sent] + send_yz(r)

    def visc_plane(i, packed):
        jump = []
        for comp in range(3):
            _, (xm, xp, ym, yp, zm, zp) = around(v0, comp, i, merged0)
            jump.append((xp - xm, yp - ym, zp - zm))
        straight = sum(jump[a][a] * jump[a][a] for a in range(3))
        skew = jnp.zeros((cy, cz), jnp.float32)
        for a, b in ((0, 1), (0, 2), (1, 2)):
            both = jump[a][b] + jump[b][a]
            skew = skew + both * both
        invariant = 1.0 + (0.125 * straight + 0.0625 * skew)
        creeping = pref_cells[i // BLOCK] * jnp.exp(jnp.log(invariant) * (-1.0 / 3.0))
        plastic = yield_cells[i // BLOCK] * lax.rsqrt(invariant)
        value = jnp.minimum(creeping, plastic)
        visc[i + 1, rows, :] = value
        visc_ref[i] = value
        return pack(1, 0, i, value, packed)

    waits = ends_first(visc_plane, 1, visc, False)

    def flag(condition):
        return jnp.where(condition, 1.0, 0.0).astype(jnp.float32)

    def restrict_planes(source, first, held, count, target, level):
        for k in range(-1, count + 1):
            total = None
            for shift, factor in ((-1, 0.125), (0, 0.375), (1, 0.375), (2, 0.125)):
                at = 2 * k + shift - first
                if 0 <= at < held:
                    term = factor * source[at, rows, :]
                    total = term if total is None else total + term
            if k == -1:
                total = total * flag(has_down[0])
                gx_send[1, level] = total
            if k == count:
                total = total * flag(has_up[0])
                gx_send[0, level] = total
            target[k + 1, rows, :] = total

    restrict_planes(visc.at[pl.ds(1, cx)], 0, cx, cx // 2, cx1, 0)
    restrict_planes(cx1, -1, cx // 2 + 2, cx // 4, cx2, 1)
    restrict_planes(cx2, -1, cx // 4 + 2, cx // 8, cx3, 2)
    wait_gx = exchange(12, 0, gx_send.at[0], gx_recv.at[0], gx_send.at[1], gx_recv.at[1])

    forc_in.wait()

    def early_one(i, carry):
        plane = visc.at[i + 1]
        centre = plane[rows, :]
        sides = (
            centre + visc[i, rows, :],
            centre + visc[i + 2, rows, :],
            centre + plane[PAD - 1 : PAD - 1 + cy, :],
            centre + plane[PAD + 1 : PAD + 1 + cy, :],
            centre + jnp.where(first_lane, 0.0, pltpu.roll(centre, 1, 1)),
            centre + jnp.where(last_lane, 0.0, pltpu.roll(centre, cz - 1, 1)),
        )
        for n, side in enumerate(sides):
            faces[n, i] = side
        diag[i] = (sides[0] + sides[1]) + (sides[2] + sides[3]) + (sides[4] + sides[5])
        for comp in range(3):
            _, near = around(v0, comp, i, merged0)
            flow = 2.0 * forc[comp, i]
            for n in range(6):
                flow = flow + sides[n] * near[n]
            early[comp, i] = flow
        return carry

    lax.fori_loop(1, cx - 1, early_one, 0)
    for wait in waits:
        wait()

    def late_one(i, carry):
        ends = ((0, 2, 0, PAD - 1), (1, 3, cy - 1, PAD + cy))
        for side, face, at, row in ends:
            halo = y_recv[1, side, 0, pl.ds(i, 1), :]
            faces[face, i, at : at + 1, :] = faces[face, i, at : at + 1, :] + halo
            diag[i, at : at + 1, :] = diag[i, at : at + 1, :] + halo
            for comp in range(3):
                near = v0[comp, i + 1, row : row + 1, :]
                early[comp, i, at : at + 1, :] = early[comp, i, at : at + 1, :] + halo * near
        return carry

    for i in (0, cx - 1):
        visc[i + 1, PAD - 1 : PAD, :] = y_recv[1, 0, 0, i : i + 1, :]
        visc[i + 1, PAD + cy : PAD + cy + 1, :] = y_recv[1, 1, 0, i : i + 1, :]
    lax.fori_loop(1, cx - 1, late_one, 0, unroll=UNROLL)
    merged1 = merged_z(1)

    def sweep_one_inner(i, packed):
        halo = pltpu.roll(merged1, cz - 1 - 2 * i, 1)
        halo = jnp.where(first_lane | last_lane, halo, 0.0)
        total = diag[i] + halo
        scale = RELAXATION / total
        diag[i] = total
        weight[i] = scale
        own = jnp.where(first_lane, faces[4, i], jnp.where(last_lane, faces[5, i], 0.0))
        z_faces[i] = own + halo
        for comp in range(3):
            edge = pltpu.roll(merged0, cz - 1 - 2 * (comp * cx + i), 1)
            flow = early[comp, i] + halo * edge
            value = (1.0 - RELAXATION) * v0[comp, i + 1, rows, :] + scale * flow
            v1[comp, i + 1, rows, :] = value
            packed = pack(2, comp, i, value, packed)
        return packed

    def sweep_one(i, packed):
        centre = visc[i + 1, rows, :]
        ym, yp, zm, zp = along(visc.at[i + 1], centre, merged1, i)
        sides = [centre + side for side in (visc[i, rows, :], visc[i + 2, rows, :], ym, yp, zm, zp)]
        total = (sides[0] + sides[1]) + (sides[2] + sides[3]) + (sides[4] + sides[5])
        scale = RELAXATION / total
        for n, side in enumerate(sides):
            faces[n, i] = side
        diag[i] = total
        weight[i] = scale
        z_faces[i] = jnp.where(first_lane, sides[4], jnp.where(last_lane, sides[5], 0.0))
        for comp in range(3):
            here, near = around(v0, comp, i, merged0)
            flow = sides[0] * near[0]
            for n in range(1, 6):
                flow = flow + sides[n] * near[n]
            value = (1.0 - RELAXATION) * here + scale * (2.0 * forc[comp, i] + flow)
            v1[comp, i + 1, rows, :] = value
            packed = pack(2, comp, i, value, packed)
        return packed

    waits = ends_first(sweep_one, 2, v1, True, sweep_one_inner)

    wait_gx()
    low_y, high_y = flag(has_down[1]), flag(has_up[1])
    gx_counts = (cx // 2, cx // 4, cx // 8)
    for level, buf in enumerate((cx1, cx2, cx3)):
        buf[1, rows, :] = buf[1, rows, :] + gx_recv[0, level]
        last = gx_counts[level]
        buf[last, rows, :] = buf[last, rows, :] + gx_recv[1, level]

    def restrict_rows(source, target, count):
        size = count + 2
        a, b, c, d = (source[pl.ds(PAD - 3 + s, size, stride=2), :] for s in range(4))
        target[PAD - 1 : PAD - 1 + size, :] = 0.125 * (a + d) + 0.375 * (b + c)
        target[PAD - 1 : PAD, :] = target[PAD - 1 : PAD, :] * low_y
        target[PAD + count : PAD + count + 1, :] = target[PAD + count : PAD + count + 1, :] * high_y

    row = 0
    ghost_rows = []
    for level, (buf, steps) in enumerate(((cx1, (t1,)), (cx2, (t2a, t2b)), (cx3, (t3a, t3b, t3c)))):
        for k in range(gx_counts[level]):
            source = buf.at[k + 1]
            for depth, target in enumerate(steps):
                restrict_rows(source, target.at[k], cy >> (depth + 1))
                source = target.at[k]
            count = cy >> len(steps)
            gy_send[1, row : row + 1, :] = source[PAD - 1 : PAD, :]
            gy_send[0, row : row + 1, :] = source[PAD + count : PAD + count + 1, :]
            ghost_rows.append((steps[-1], k, count, row))
            row += 1
    wait_gy = exchange(13, 1, gy_send.at[0], gy_recv.at[0], gy_send.at[1], gy_recv.at[1])

    def early_flow(buf):
        def body(i, carry):
            for comp in range(3):
                plane = buf.at[comp, i + 1]
                centre = plane[rows, :]
                low = jnp.where(first_lane, 0.0, pltpu.roll(centre, 1, 1))
                high = jnp.where(last_lane, 0.0, pltpu.roll(centre, cz - 1, 1))
                flow = 2.0 * forc[comp, i]
                flow = flow + faces[0, i] * buf[comp, i, rows, :]
                flow = flow + faces[1, i] * buf[comp, i + 2, rows, :]
                flow = flow + faces[2, i] * plane[PAD - 1 : PAD - 1 + cy, :]
                flow = flow + faces[3, i] * plane[PAD + 1 : PAD + 1 + cy, :]
                early[comp, i] = flow + (faces[4, i] * low + faces[5, i] * high)
            return carry

        lax.fori_loop(1, cx - 1, body, 0)

    def late_rows(r, buf):
        def body(i, carry):
            for comp in range(3):
                low = faces[2, i, 0:1, :] * y_recv[r, 0, comp, pl.ds(i, 1), :]
                high = faces[3, i, cy - 1 : cy, :] * y_recv[r, 1, comp, pl.ds(i, 1), :]
                early[comp, i, 0:1, :] = early[comp, i, 0:1, :] + low
                early[comp, i, cy - 1 : cy, :] = early[comp, i, cy - 1 : cy, :] + high
            return carry

        for i in (0, cx - 1):
            for comp in range(3):
                buf[comp, i + 1, PAD - 1 : PAD, :] = y_recv[r, 0, comp, i : i + 1, :]
                buf[comp, i + 1, PAD + cy : PAD + cy + 1, :] = y_recv[r, 1, comp, i : i + 1, :]
        lax.fori_loop(1, cx - 1, body, 0, unroll=UNROLL)

    def late(comp, i, merged):
        edge = pltpu.roll(merged, cz - 1 - 2 * (comp * cx + i), 1)
        return early[comp, i] + z_faces[i] * edge

    early_flow(v1)
    for wait in waits:
        wait()
    late_rows(2, v1)
    merged2 = merged_z(2)

    def flow_of(buf, comp, i, merged):
        here, near = around(buf, comp, i, merged)
        flow = faces[0, i] * near[0]
        for n in range(1, 6):
            flow = flow + faces[n, i] * near[n]
        return here, flow

    def sweep_two_inner(i, packed):
        for comp in range(3):
            value = (1.0 - RELAXATION) * v1[comp, i + 1, rows, :] + weight[i] * late(comp, i, merged2)
            v2[comp, i + 1, rows, :] = value
            smooth_ref[comp, i] = value
            packed = pack(3, comp, i, value, packed)
        return packed

    def sweep_two(i, packed):
        for comp in range(3):
            here, flow = flow_of(v1, comp, i, merged2)
            value = (1.0 - RELAXATION) * here + weight[i] * (2.0 * forc[comp, i] + flow)
            v2[comp, i + 1, rows, :] = value
            smooth_ref[comp, i] = value
            packed = pack(3, comp, i, value, packed)
        return packed

    waits = ends_first(sweep_two, 3, v2, True, sweep_two_inner)

    wait_gy()
    for buf, k, count, row in ghost_rows:
        buf[k, PAD : PAD + 1, :] = buf[k, PAD : PAD + 1, :] + gy_recv[0, row : row + 1, :]
        last = PAD + count - 1
        buf[k, last : last + 1, :] = buf[k, last : last + 1, :] + gy_recv[1, row : row + 1, :]
    mats_in.wait()
    off_low, off_high = 1.0 - flag(has_down[2]), 1.0 - flag(has_up[2])
    results = []
    groups = []
    lane8 = lax.broadcasted_iota(jnp.int32, (8, cz), 1)
    packed = jnp.zeros((8, cz), jnp.float32)
    for level, buf in enumerate((t1, t2b, t3c)):
        count = gx_counts[level]
        height = max(8, cy >> (level + 1))
        matrix = mats[0, level] - off_low * mats[1, level] - off_high * mats[2, level]
        data = buf[:, PAD : PAD + height, :].reshape(count * height, cz)
        result = jnp.dot(data, matrix, preferred_element_type=jnp.float32, precision=HIGHEST)
        for part in range(count * height // 8):
            g = len(groups)
            piece = result[8 * part : 8 * part + 8, :]
            groups.append((level, 8 * part // height, 8 * part % height, piece))
            shifted = pltpu.roll(piece, (2 * g - GHOST) % cz, 1)
            packed = jnp.where((lane8 == 2 * g) | (lane8 == 2 * g + 1), shifted, packed)
    gz_send[...] = packed
    wait_gz = exchange(14, 2, gz_send, gz_recv.at[0], gz_send, gz_recv.at[1])

    early_flow(v2)
    for wait in waits:
        wait()
    late_rows(3, v2)
    merged3 = merged_z(3)

    def misfit_plane(i, total):
        for comp in range(3):
            here, flow = flow_of(v2, comp, i, merged3)
            value = forc[comp, i] + 0.5 * (flow - diag[i] * here)
            misfit_ref[comp, i] = value
            total = total + value * value
        return total

    def misfit_inner(i, total):
        for comp in range(3):
            value = 0.5 * (late(comp, i, merged3) - diag[i] * v2[comp, i + 1, rows, :])
            misfit_ref[comp, i] = value
            total = total + value * value
        return total

    squares = lax.fori_loop(0, 2, lambda t, carry: misfit_plane(t * (cx - 1), carry), nothing)
    squares = lax.fori_loop(1, cx - 1, misfit_inner, squares, unroll=UNROLL)
    part = jnp.sum(squares, axis=0, keepdims=True)

    def gather(slots, mine, value, peers, sends, recvs):
        slots[mine] = value
        copies = []
        for k, peer in enumerate(peers):
            copy = pltpu.make_async_remote_copy(
                slots.at[mine], slots.at[mine], sends.at[k], recvs.at[k],
                device_id=peer, device_id_type=MESH,
            )
            copy.start()
            copies.append(copy)
        return copies

    def total_of(slots):
        total = slots[0]
        for n in range(1, slots.shape[0]):
            total = total + slots[n]
        return total

    plane_copies = gather(sums_xy, me_first, part, plane_peers, plane_send, plane_recv)

    wait_gz()
    low_part, high_part = gz_recv[0], gz_recv[1]
    for g, (level, k, at, piece) in enumerate(groups):
        width = cz >> (level + 1)
        height = cy >> (level + 1)
        piece = piece + jnp.where(lane8 == 0, pltpu.roll(low_part, (cz - 2 * g - 1) % cz, 1), 0.0)
        piece = piece + jnp.where(
            lane8 == width - 1, pltpu.roll(high_part, (width - 1 - 2 * g) % cz, 1), 0.0
        )
        target = (one_ref, two_ref, three_ref)[level]
        size = min(8, height - at)
        target[k, at : at + size, :] = piece[:size, :width]

    for copy in plane_copies:
        copy.wait()
    whole = total_of(sums_xy)
    if not one_stage:
        line_copies = gather(sums_z, iz, whole, line_peers, line_send, line_recv)
        for copy in line_copies:
            copy.wait()
        whole = total_of(sums_z)
    whole = jnp.sum(whole, axis=1, keepdims=True)
    cells_all = float(3 * cx * nx * cy * ny * cz * nz)
    rms_ref[...] = jnp.sqrt(whole / cells_all)

    for condition, copy in started:
        pl.when(condition)(copy.wait_send)


def writer(*refs):
    copies = [
        pltpu.make_async_copy(refs[n], refs[7 + n], refs[14].at[n]) for n in (0, 5, 1, 2, 3, 4, 6)
    ]
    for copy in copies:
        copy.start()
    for copy in copies:
        copy.wait()


def per_device(velocity, forcing, phase_block, prefactor, yield_stress):
    _, cx, cy, cz = velocity.shape
    nx, ny, nz = lax.axis_size("gx"), lax.axis_size("gy"), lax.axis_size("gz")
    f32 = jnp.float32
    sizes = (nx, ny, nz, cx, cy, cz, prefactor.shape[0])
    mats = jnp.asarray(coarse_matrices(cz))
    blocks = phase_block.reshape(phase_block.shape[0] * phase_block.shape[1], phase_block.shape[2])
    tall = cy + 2 * PAD
    firsts = nx * ny * nz if nx * ny * nz <= ONE_STAGE else nx * ny
    ghosts = cx // 2 + cx // 4 + cx // 8
    ghosts += -ghosts % 8
    hbm = pl.BlockSpec(memory_space=pltpu.HBM)
    vmem = pl.BlockSpec(memory_space=pltpu.VMEM)
    v = pltpu.VMEM
    field = v((3, cx + 2, tall, cz), f32)
    dma = pltpu.SemaphoreType.DMA
    operands = (velocity, forcing, mats, blocks, prefactor, yield_stress)
    outs = pl.pallas_call(
        functools.partial(kernel, sizes),
        out_shape=(
            jax.ShapeDtypeStruct(velocity.shape, f32),
            jax.ShapeDtypeStruct((cx, cy, cz), f32),
            jax.ShapeDtypeStruct((cx // 2, cy // 2, cz // 2), f32),
            jax.ShapeDtypeStruct((cx // 4, cy // 4, cz // 4), f32),
            jax.ShapeDtypeStruct((cx // 8, cy // 8, cz // 8), f32),
            jax.ShapeDtypeStruct(velocity.shape, f32),
            jax.ShapeDtypeStruct((1, 1), f32),
        ),
        in_specs=[hbm] * 6,
        out_specs=(vmem,) * 7,
        scratch_shapes=[
            field,
            field,
            field,
            v((cx + 2, tall, cz), f32),
            v((3, cx, cy, cz), f32),
            v(mats.shape, f32),
            v(blocks.shape, blocks.dtype),
            pltpu.SMEM(prefactor.shape, f32),
            pltpu.SMEM(yield_stress.shape, f32),
            v((6, cx, cy, cz), f32),
            v((cx, cy, cz), f32),
            v((3, cx, cy, cz), f32),
            v((cx, cy, cz), f32),
            v((cx, cy, cz), f32),
            v((cx // BLOCK, cy, cz), f32),
            v((cx // BLOCK, cy, cz), f32),
            v((4, 2, 3, cx, cz), f32),
            v((4, 2, 3, cx, cz), f32),
            v((4, cy, cz), f32),
            v((4, 2, cy, cz), f32),
            v((cx // 2 + 2, tall, cz), f32),
            v((cx // 4 + 2, tall, cz), f32),
            v((cx // 8 + 2, tall, cz), f32),
            v((2, 3, cy, cz), f32),
            v((2, 3, cy, cz), f32),
            v((cx // 2, tall, cz), f32),
            v((cx // 4, tall, cz), f32),
            v((cx // 4, tall, cz), f32),
            v((cx // 8, tall, cz), f32),
            v((cx // 8, tall, cz), f32),
            v((cx // 8, tall, cz), f32),
            v((2, ghosts, cz), f32),
            v((2, ghosts, cz), f32),
            v((8, cz), f32),
            v((2, 8, cz), f32),
            v((firsts, 1, cz), f32),
            v((nz, 1, cz), f32),
            dma((6,)),
            dma((15, 2)),
            dma((15, 2)),
            dma((firsts - 1,)),
            dma((firsts - 1,)),
            dma((nz - 1,)),
            dma((nz - 1,)),
        ],
        compiler_params=pltpu.CompilerParams(
            collective_id=0, has_side_effects=True, vmem_limit_bytes=40 * 1024 * 1024
        ),
    )(*(pltpu.with_memory_space_constraint(a, pltpu.HBM) for a in operands))
    outs = pl.pallas_call(
        writer,
        out_shape=tuple(jax.ShapeDtypeStruct(out.shape, f32) for out in outs),
        in_specs=[vmem] * 7,
        out_specs=(hbm,) * 7,
        scratch_shapes=[dma((7,))],
        compiler_params=pltpu.CompilerParams(vmem_limit_bytes=8 * 1024 * 1024),
    )(*outs)
    return outs[:6] + (outs[6].reshape(()),)


def solution(mesh):
    grid = P("gx", "gy", "gz")
    vector = P(None, "gx", "gy", "gz")
    return jax.shard_map(
        per_device,
        mesh=mesh,
        in_specs=(vector, vector, grid, P(), P()),
        out_specs=(vector, grid, grid, grid, grid, vector, P()),
        check_vma=False,
    )
```

profile of v0, /device:TPU:0, one launch (start us, length us, event | category | flops | bytes accessed | tf_op | source)
XLA Modules:
  0.0 34.0 jit_solution(6643620544313081433)
XLA Ops:
  0.6 31.4 %shard_map.117 = (f32[3,16,32,128]{3,2,1,0:T(8,128)S(1)}, f32[16,32,128]{2,1,0:T(8,128)S(1)}, f32[8,16,64]{2,1,0:T(8,128)S(1)}, f32[4,8,32]{2,1,0:T(8,128)S(1)},...) custom-call(f32[3,16,32,128]{3,2,1,0:T(8,128)} %vel_hbm.1, f32[3,16,32,128]{3,2,1,0:T(8,128)} %forc_hbm.1, ...), custom_call_target="tpu_custom_call" | custom-call | tf_op jit(solution)/shard_map/pallas_call | solution.py:668
  32.1 1.9 %shard_map.118 = (f32[3,16,32,128]{3,2,1,0:T(8,128)}, f32[16,32,128]{2,1,0:T(8,128)}, f32[8,16,64]{2,1,0:T(8,128)}, f32[4,8,32]{2,1,0:T(8,128)}, f32[2,4,16]{2,1...) custom-call(f32[3,16,32,128]{3,2,1,0:T(8,128)S(1)} %get-tuple-element.21.refs_0_, ...), custom_call_target="tpu_custom_call" | custom-call | tf_op jit(solution)/shard_map/pallas_call | solution.py:731
where the time goes:
time: 34.2 us; the launch traced here: 34 us
  Pallas kernels  33.4 us (98%)
  between operations  0.64 us (2%)
    pallas_call x1, Pallas kernels, per_device(): pl.pallas_call(functools.partial(kernel, sizes), out_shape=(jax.ShapeDtyp...  31.4 us
    pallas_call x1, Pallas kernels, per_device(): pl.pallas_call(writer, out_shape=tuple((jax.ShapeDtypeStruct(out.shape, f...  1.93 us

commit v1 on v0

--- a/solution.py
+++ b/solution.py
@@ -12,8 +12,9 @@
 RELAXATION = 0.8
 PAD = 8
 GHOST = 64
-UNROLL = 2
+UNROLL = 7
 ONE_STAGE = 32
+ROUNDS = 4
 MESH = pl.DeviceIdType.MESH
 HIGHEST = lax.Precision.HIGHEST
 
@@ -159,7 +160,14 @@
             other = lax.rem(me_xy + k, nx * ny)
             plane_peers.append((other // ny, lax.rem(other, ny), iz))
         line_peers = [(ix, iy, lax.rem(iz + k, nz)) for k in range(1, nz)]
-    for peer in plane_peers + line_peers:
+    steps = [nx - 1, ny - 1, nz - 1] if one_stage else [nx - 1, ny - 1]
+    if sum(steps) - max(steps) <= ROUNDS:
+        greeted = [(lax.rem(ix + k, nx), iy, iz) for k in range(1, nx)]
+        greeted += [(ix, lax.rem(iy + k, ny), iz) for k in range(1, ny)]
+        greeted += [(ix, iy, lax.rem(iz + k, nz)) for k in range(1, nz)]
+    else:
+        greeted = plane_peers + line_peers
+    for peer in greeted:
         pl.semaphore_signal(barrier, inc=1, device_id=peer, device_id_type=MESH)
 
     lane = lax.broadcasted_iota(jnp.int32, (cy, cz), 1)
@@ -268,7 +276,7 @@
 
     nothing = jnp.zeros((cy, cz), jnp.float32)
     z_send[0] = lax.fori_loop(0, cx, pack_first, nothing, unroll=UNROLL)
-    pl.semaphore_wait(barrier, len(plane_peers) + len(line_peers))
+    pl.semaphore_wait(barrier, len(greeted))
     waits = [send_x(0, v0, True)] + send_yz(0)
 
     phase_in.wait()
@@ -379,7 +387,7 @@
             early[comp, i] = flow
         return carry
 
-    lax.fori_loop(1, cx - 1, early_one, 0)
+    lax.fori_loop(1, cx - 1, early_one, 0, unroll=UNROLL)
     for wait in waits:
         wait()
 
@@ -485,7 +493,7 @@
                 early[comp, i] = flow + (faces[4, i] * low + faces[5, i] * high)
             return carry
 
-        lax.fori_loop(1, cx - 1, body, 0)
+        lax.fori_loop(1, cx - 1, body, 0, unroll=UNROLL)
 
     def late_rows(r, buf):
         def body(i, carry):

time: 34.2 us -> 32.4 us (0.947)
  Pallas kernels: 33.4 us -> 31.6 us
    pallas_call x1, Pallas kernels: 31.4 us -> 29.7 us  [per_device(): pl.pallas_call(functools.partial(kernel, sizes), out_shape=(jax.ShapeDtyp...]
where the time goes in v1:
time: 32.4 us; the launch traced here: 32.2 us
  Pallas kernels  31.6 us (98%)
  between operations  0.64 us (2%)
    pallas_call x1, Pallas kernels, per_device(): pl.pallas_call(functools.partial(kernel, sizes), out_shape=(jax.ShapeDtyp...  29.7 us
    pallas_call x1, Pallas kernels, per_device(): pl.pallas_call(writer, out_shape=tuple((jax.ShapeDtypeStruct(out.shape, f...  1.93 us

profile of v1, /device:TPU:0, one launch (start us, length us, event | category | flops | bytes accessed | tf_op | source)
XLA Modules:
  0.0 32.2 jit_solution(1795898987940418545)
XLA Ops:
  0.6 29.7 %shard_map.117 = (f32[3,16,32,128]{3,2,1,0:T(8,128)S(1)}, f32[16,32,128]{2,1,0:T(8,128)S(1)}, f32[8,16,64]{2,1,0:T(8,128)S(1)}, f32[4,8,32]{2,1,0:T(8,128)S(1)},...) custom-call(f32[3,16,32,128]{3,2,1,0:T(8,128)} %vel_hbm.1, f32[3,16,32,128]{3,2,1,0:T(8,128)} %forc_hbm.1, ...), custom_call_target="tpu_custom_call" | custom-call | tf_op jit(solution)/shard_map/pallas_call | solution.py:676
  30.3 1.9 %shard_map.118 = (f32[3,16,32,128]{3,2,1,0:T(8,128)}, f32[16,32,128]{2,1,0:T(8,128)}, f32[8,16,64]{2,1,0:T(8,128)}, f32[4,8,32]{2,1,0:T(8,128)}, f32[2,4,16]{2,1...) custom-call(f32[3,16,32,128]{3,2,1,0:T(8,128)S(1)} %get-tuple-element.21.refs_0_, ...), custom_call_target="tpu_custom_call" | custom-call | tf_op jit(solution)/shard_map/pallas_call | solution.py:739

commit v2 on v1

--- a/solution.py
+++ b/solution.py
@@ -12,7 +12,11 @@
 RELAXATION = 0.8
 PAD = 8
 GHOST = 64
-UNROLL = 7
+UNROLL = 4
+VISC_UNROLL = 7
+TILE = 8
+AHEAD = 2
+BEHIND = 2
 ONE_STAGE = 32
 ROUNDS = 4
 MESH = pl.DeviceIdType.MESH
@@ -75,11 +79,15 @@
     yield_ref,
     faces,
     z_faces,
+    z_scaled,
     early,
     weight,
     diag,
     pref_cells,
     yield_cells,
+    x_send,
+    x_recv,
+    visc_x,
     y_send,
     y_recv,
     z_send,
@@ -117,8 +125,6 @@
     forc_in = pltpu.make_async_copy(forc_hbm, forc, local_sem.at[1])
     mats_in = pltpu.make_async_copy(mats_hbm, mats, local_sem.at[2])
     vel_in.start()
-    forc_in.start()
-    mats_in.start()
     phase_in = pltpu.make_async_copy(phase_hbm, phase_ref, local_sem.at[3])
     phase_in.start()
     pref_in = pltpu.make_async_copy(pref_hbm, pref_ref, local_sem.at[4])
@@ -138,6 +144,8 @@
         buf[:, 1 : cx + 1, PAD + cy : PAD + cy + 1, :] = row0
     visc[0, rows, :] = plane0[0]
     visc[cx + 1, rows, :] = plane0[0]
+    x_recv[...] = jnp.zeros(x_recv.shape, jnp.float32)
+    visc_x[...] = jnp.zeros(visc_x.shape, jnp.float32)
     y_recv[...] = jnp.zeros(y_recv.shape, jnp.float32)
     z_recv[...] = jnp.zeros(z_recv.shape, jnp.float32)
     gx_recv[...] = jnp.zeros(gx_recv.shape, jnp.float32)
@@ -172,8 +180,10 @@
 
     lane = lax.broadcasted_iota(jnp.int32, (cy, cz), 1)
     odd_lane = lax.rem(lane, 2) == 1
+    lane_pair = (lane - 1) // 2
     first_lane = lane == 0
     last_lane = lane == cz - 1
+    end_lane = first_lane | last_lane
 
     up_ids = (
         (lax.rem(ix + 1, nx), iy, iz),
@@ -209,18 +219,8 @@
 
         return wait
 
-    def send_x(r, buf, vector):
-        if vector:
-            return exchange(
-                3 * r, 0,
-                buf.at[:, cx, rows, :], buf.at[:, 0, rows, :],
-                buf.at[:, 1, rows, :], buf.at[:, cx + 1, rows, :],
-            )
-        return exchange(
-            3 * r, 0,
-            buf.at[cx, rows, :], buf.at[0, rows, :],
-            buf.at[1, rows, :], buf.at[cx + 1, rows, :],
-        )
+    def send_x(r, last, low, first, high):
+        return exchange(3 * r, 0, last, low, first, high)
 
     def send_yz(r):
         held = pl.ds(0, 1 if r == 1 else 3)
@@ -237,8 +237,7 @@
         y_send[r, 0, comp, pl.ds(i, 1), :] = value[cy - 1 : cy, :]
         y_send[r, 1, comp, pl.ds(i, 1), :] = value[0:1, :]
         place = 2 * (comp * cx + i) + 1
-        here = (lane == place) | (lane == place + 1)
-        return jnp.where(here, pltpu.roll(value, place + 1, 1), packed)
+        return jnp.where(lane_pair == comp * cx + i, pltpu.roll(value, place + 1, 1), packed)
 
     def unpack_y(r, buf, comps):
         def body(i, carry):
@@ -268,16 +267,17 @@
         return centre, (buf[comp, i, rows, :], buf[comp, i + 2, rows, :], ym, yp, zm, zp)
 
     vel_in.wait()
-
-    def pack_first(i, packed):
+    forc_in.start()
+    mats_in.start()
+
+    nothing = jnp.zeros((cy, cz), jnp.float32)
+    packed = nothing
+    for i in range(cx):
         for comp in range(3):
             packed = pack(0, comp, i, v0[comp, i + 1, rows, :], packed)
-        return packed
-
-    nothing = jnp.zeros((cy, cz), jnp.float32)
-    z_send[0] = lax.fori_loop(0, cx, pack_first, nothing, unroll=UNROLL)
+    z_send[0] = packed
     pl.semaphore_wait(barrier, len(greeted))
-    waits = [send_x(0, v0, True)] + send_yz(0)
+    waits = [send_x(0, v0.at[:, cx, rows, :], v0.at[:, 0, rows, :], v0.at[:, 1, rows, :], v0.at[:, cx + 1, rows, :])] + send_yz(0)
 
     phase_in.wait()
     pref_in.wait()
@@ -313,31 +313,79 @@
     unpack_y(0, v0, 3)
     merged0 = merged_z(0)
 
-    def ends_first(body, r, buf, vector, inner=None):
-        packed = lax.fori_loop(0, 2, lambda t, carry: body(t * (cx - 1), carry), nothing)
-        sent = send_x(r, buf, vector)
-        z_send[r] = lax.fori_loop(1, cx - 1, inner or body, packed, unroll=UNROLL)
+    order = [0, cx - 1] + list(range(1, cx - 1))
+
+    def shell_pass(edge, value_of, r, send_ends, vector=True):
+        comps = 3 if vector else 1
+        packed = nothing
+        edges, rolled = {}, {}
+        sent = None
+        for t in range(cx + AHEAD + BEHIND):
+            if t < cx:
+                edges[t] = edge(order[t])
+            n = t - AHEAD
+            if 0 <= n < cx:
+                i = order[n]
+                moved = []
+                for comp, value in enumerate(value_of(i, edges.pop(n))):
+                    if r is not None:
+                        y_send[r, 0, comp, pl.ds(i, 1), :] = value[cy - 1 : cy, :]
+                        y_send[r, 1, comp, pl.ds(i, 1), :] = value[0:1, :]
+                        moved.append((comp * cx + i, pltpu.roll(value, 2 * (comp * cx + i) + 2, 1)))
+                rolled[n] = moved
+                if n == 1 and send_ends is not None:
+                    sent = send_ends()
+            n = t - AHEAD - BEHIND
+            if 0 <= n < cx:
+                for place, value in rolled.pop(n):
+                    packed = jnp.where(lane_pair == place, value, packed)
+        if r is None:
+            return None
+        z_send[r] = packed
         return [sent] + send_yz(r)
 
-    def visc_plane(i, packed):
+    def edge_of(merged, place):
+        return pltpu.roll(merged, cz - 1 - 2 * place, 1)
+
+    def visc_plane(i, carry):
+        packed, held, at = carry
+        out = []
+        centres = [v0[comp, i + 1, rows, :] for comp in range(3)]
+        edges = [edge_of(merged0, comp * cx + i) for comp in range(3)]
+        lows = [pltpu.roll(centre, 1, 1) for centre in centres]
+        highs = [pltpu.roll(centre, cz - 1, 1) for centre in centres]
+        moved = pltpu.roll(held, 2 * at + 2, 1)
+        packed = jnp.where(lane_pair == at, moved, packed)
         jump = []
         for comp in range(3):
-            _, (xm, xp, ym, yp, zm, zp) = around(v0, comp, i, merged0)
-            jump.append((xp - xm, yp - ym, zp - zm))
+            plane = v0.at[comp, i + 1]
+            below = jnp.where(first_lane, edges[comp], lows[comp])
+            above = jnp.where(last_lane, edges[comp], highs[comp])
+            jump.append((
+                v0[comp, i + 2, rows, :] - v0[comp, i, rows, :],
+                plane[PAD + 1 : PAD + 1 + cy, :] - plane[PAD - 1 : PAD - 1 + cy, :],
+                above - below,
+            ))
         straight = sum(jump[a][a] * jump[a][a] for a in range(3))
-        skew = jnp.zeros((cy, cz), jnp.float32)
+        skew = None
         for a, b in ((0, 1), (0, 2), (1, 2)):
             both = jump[a][b] + jump[b][a]
-            skew = skew + both * both
+            skew = both * both if skew is None else skew + both * both
         invariant = 1.0 + (0.125 * straight + 0.0625 * skew)
         creeping = pref_cells[i // BLOCK] * jnp.exp(jnp.log(invariant) * (-1.0 / 3.0))
         plastic = yield_cells[i // BLOCK] * lax.rsqrt(invariant)
         value = jnp.minimum(creeping, plastic)
         visc[i + 1, rows, :] = value
         visc_ref[i] = value
-        return pack(1, 0, i, value, packed)
-
-    waits = ends_first(visc_plane, 1, visc, False)
+        y_send[1, 0, 0, pl.ds(i, 1), :] = value[cy - 1 : cy, :]
+        y_send[1, 1, 0, pl.ds(i, 1), :] = value[0:1, :]
+        return packed, value, i
+
+    carry = visc_plane(cx - 1, visc_plane(0, (nothing, nothing, 0)))
+    sent = send_x(1, visc.at[cx, rows, :], visc_x.at[0], visc.at[1, rows, :], visc_x.at[1])
+    packed, held, at = lax.fori_loop(1, cx - 1, visc_plane, carry, unroll=VISC_UNROLL)
+    z_send[1] = jnp.where(lane_pair == at, pltpu.roll(held, 2 * at + 2, 1), packed)
+    waits = [sent] + send_yz(1)
 
     def flag(condition):
         return jnp.where(condition, 1.0, 0.0).astype(jnp.float32)
@@ -376,8 +424,10 @@
             centre + jnp.where(first_lane, 0.0, pltpu.roll(centre, 1, 1)),
             centre + jnp.where(last_lane, 0.0, pltpu.roll(centre, cz - 1, 1)),
         )
-        for n, side in enumerate(sides):
-            faces[n, i] = side
+        for n in range(4):
+            faces[n, i] = sides[n]
+        faces[4, i] = jnp.where(first_lane, 0.0, sides[4])
+        faces[5, i] = jnp.where(last_lane, 0.0, sides[5])
         diag[i] = (sides[0] + sides[1]) + (sides[2] + sides[3]) + (sides[4] + sides[5])
         for comp in range(3):
             _, near = around(v0, comp, i, merged0)
@@ -387,9 +437,17 @@
             early[comp, i] = flow
         return carry
 
-    lax.fori_loop(1, cx - 1, early_one, 0, unroll=UNROLL)
+    lax.fori_loop(0, cx, early_one, 0, unroll=UNROLL)
     for wait in waits:
         wait()
+    merged1 = merged_z(1)
+
+    for side, i, face, halo_plane in ((0, 0, 0, 0), (1, cx - 1, 1, cx + 1)):
+        halo = visc_x[side]
+        faces[face, i] = faces[face, i] + halo
+        diag[i] = diag[i] + halo
+        for comp in range(3):
+            early[comp, i] = early[comp, i] + halo * v0[comp, halo_plane, rows, :]
 
     def late_one(i, carry):
         ends = ((0, 2, 0, PAD - 1), (1, 3, cy - 1, PAD + cy))
@@ -402,51 +460,36 @@
                 early[comp, i, at : at + 1, :] = early[comp, i, at : at + 1, :] + halo * near
         return carry
 
-    for i in (0, cx - 1):
-        visc[i + 1, PAD - 1 : PAD, :] = y_recv[1, 0, 0, i : i + 1, :]
-        visc[i + 1, PAD + cy : PAD + cy + 1, :] = y_recv[1, 1, 0, i : i + 1, :]
-    lax.fori_loop(1, cx - 1, late_one, 0, unroll=UNROLL)
-    merged1 = merged_z(1)
-
-    def sweep_one_inner(i, packed):
-        halo = pltpu.roll(merged1, cz - 1 - 2 * i, 1)
-        halo = jnp.where(first_lane | last_lane, halo, 0.0)
+    lax.fori_loop(0, cx, late_one, 0, unroll=UNROLL)
+
+    def edges_one(i):
+        return [edge_of(merged1, i)] + [edge_of(merged0, comp * cx + i) for comp in range(3)]
+
+    def values_one(i, edges):
+        halo = jnp.where(end_lane, edges[0], 0.0)
         total = diag[i] + halo
         scale = RELAXATION / total
         diag[i] = total
         weight[i] = scale
-        own = jnp.where(first_lane, faces[4, i], jnp.where(last_lane, faces[5, i], 0.0))
-        z_faces[i] = own + halo
+        z_faces[i] = jnp.where(end_lane, visc[i + 1, rows, :] + halo, 0.0)
         for comp in range(3):
-            edge = pltpu.roll(merged0, cz - 1 - 2 * (comp * cx + i), 1)
-            flow = early[comp, i] + halo * edge
+            flow = early[comp, i] + halo * edges[1 + comp]
             value = (1.0 - RELAXATION) * v0[comp, i + 1, rows, :] + scale * flow
             v1[comp, i + 1, rows, :] = value
-            packed = pack(2, comp, i, value, packed)
-        return packed
-
-    def sweep_one(i, packed):
-        centre = visc[i + 1, rows, :]
-        ym, yp, zm, zp = along(visc.at[i + 1], centre, merged1, i)
-        sides = [centre + side for side in (visc[i, rows, :], visc[i + 2, rows, :], ym, yp, zm, zp)]
-        total = (sides[0] + sides[1]) + (sides[2] + sides[3]) + (sides[4] + sides[5])
-        scale = RELAXATION / total
-        for n, side in enumerate(sides):
-            faces[n, i] = side
-        diag[i] = total
-        weight[i] = scale
-        z_faces[i] = jnp.where(first_lane, sides[4], jnp.where(last_lane, sides[5], 0.0))
-        for comp in range(3):
-            here, near = around(v0, comp, i, merged0)
-            flow = sides[0] * near[0]
-            for n in range(1, 6):
-                flow = flow + sides[n] * near[n]
-            value = (1.0 - RELAXATION) * here + scale * (2.0 * forc[comp, i] + flow)
-            v1[comp, i + 1, rows, :] = value
-            packed = pack(2, comp, i, value, packed)
-        return packed
-
-    waits = ends_first(sweep_one, 2, v1, True, sweep_one_inner)
+            keep_end(2, comp, i, value)
+            yield value
+
+    def send_ends(r):
+        s = r - 2
+        return lambda: send_x(r, x_send.at[s, 0], x_recv.at[s, 0], x_send.at[s, 1], x_recv.at[s, 1])
+
+    def keep_end(r, comp, i, value):
+        if i == cx - 1:
+            x_send[r - 2, 0, comp] = value
+        if i == 0:
+            x_send[r - 2, 1, comp] = value
+
+    waits = shell_pass(edges_one, values_one, 2, send_ends(2))
 
     wait_gx()
     low_y, high_y = flag(has_down[1]), flag(has_up[1])
@@ -478,73 +521,70 @@
             row += 1
     wait_gy = exchange(13, 1, gy_send.at[0], gy_recv.at[0], gy_send.at[1], gy_recv.at[1])
 
-    def early_flow(buf):
+    def around_inner(buf, comp, i):
+        plane = buf.at[comp, i + 1]
+        centre = plane[rows, :]
+        return centre, (
+            buf[comp, i, rows, :],
+            buf[comp, i + 2, rows, :],
+            plane[PAD - 1 : PAD - 1 + cy, :],
+            plane[PAD + 1 : PAD + 1 + cy, :],
+            pltpu.roll(centre, 1, 1),
+            pltpu.roll(centre, cz - 1, 1),
+        )
+
+    def flow_inner(buf, comp, i):
+        centre, near = around_inner(buf, comp, i)
+        flow = 2.0 * forc[comp, i]
+        for n in range(6):
+            flow = flow + faces[n, i] * near[n]
+        return centre, flow
+
+    def early_two(i, carry):
+        z_scaled[i] = weight[i] * z_faces[i]
+        for comp in range(3):
+            centre, flow = flow_inner(v1, comp, i)
+            early[comp, i] = (1.0 - RELAXATION) * centre + weight[i] * flow
+        return carry
+
+    def late_ends(r, scaled):
+        for side, i, face in ((0, 0, 0), (1, cx - 1, 1)):
+            factor = faces[face, i]
+            if scaled:
+                factor = factor * weight[i]
+            for comp in range(3):
+                early[comp, i] = early[comp, i] + factor * x_recv[r - 2, side, comp]
+
         def body(i, carry):
-            for comp in range(3):
-                plane = buf.at[comp, i + 1]
-                centre = plane[rows, :]
-                low = jnp.where(first_lane, 0.0, pltpu.roll(centre, 1, 1))
-                high = jnp.where(last_lane, 0.0, pltpu.roll(centre, cz - 1, 1))
-                flow = 2.0 * forc[comp, i]
-                flow = flow + faces[0, i] * buf[comp, i, rows, :]
-                flow = flow + faces[1, i] * buf[comp, i + 2, rows, :]
-                flow = flow + faces[2, i] * plane[PAD - 1 : PAD - 1 + cy, :]
-                flow = flow + faces[3, i] * plane[PAD + 1 : PAD + 1 + cy, :]
-                early[comp, i] = flow + (faces[4, i] * low + faces[5, i] * high)
+            for side, face, at in ((0, 2, 0), (1, 3, cy - 1)):
+                factor = faces[face, i, at : at + 1, :]
+                if scaled:
+                    factor = factor * weight[i, at : at + 1, :]
+                for comp in range(3):
+                    halo = y_recv[r, side, comp, pl.ds(i, 1), :]
+                    early[comp, i, at : at + 1, :] = early[comp, i, at : at + 1, :] + factor * halo
             return carry
 
-        lax.fori_loop(1, cx - 1, body, 0, unroll=UNROLL)
-
-    def late_rows(r, buf):
-        def body(i, carry):
-            for comp in range(3):
-                low = faces[2, i, 0:1, :] * y_recv[r, 0, comp, pl.ds(i, 1), :]
-                high = faces[3, i, cy - 1 : cy, :] * y_recv[r, 1, comp, pl.ds(i, 1), :]
-                early[comp, i, 0:1, :] = early[comp, i, 0:1, :] + low
-                early[comp, i, cy - 1 : cy, :] = early[comp, i, cy - 1 : cy, :] + high
-            return carry
-
-        for i in (0, cx - 1):
-            for comp in range(3):
-                buf[comp, i + 1, PAD - 1 : PAD, :] = y_recv[r, 0, comp, i : i + 1, :]
-                buf[comp, i + 1, PAD + cy : PAD + cy + 1, :] = y_recv[r, 1, comp, i : i + 1, :]
-        lax.fori_loop(1, cx - 1, body, 0, unroll=UNROLL)
-
-    def late(comp, i, merged):
-        edge = pltpu.roll(merged, cz - 1 - 2 * (comp * cx + i), 1)
-        return early[comp, i] + z_faces[i] * edge
-
-    early_flow(v1)
+        lax.fori_loop(0, cx, body, 0, unroll=UNROLL)
+
+    lax.fori_loop(0, cx, early_two, 0, unroll=UNROLL)
     for wait in waits:
         wait()
-    late_rows(2, v1)
     merged2 = merged_z(2)
-
-    def flow_of(buf, comp, i, merged):
-        here, near = around(buf, comp, i, merged)
-        flow = faces[0, i] * near[0]
-        for n in range(1, 6):
-            flow = flow + faces[n, i] * near[n]
-        return here, flow
-
-    def sweep_two_inner(i, packed):
+    late_ends(2, True)
+
+    def edges_two(i):
+        return [edge_of(merged2, comp * cx + i) for comp in range(3)]
+
+    def values_two(i, edges):
+        factor = z_scaled[i]
         for comp in range(3):
-            value = (1.0 - RELAXATION) * v1[comp, i + 1, rows, :] + weight[i] * late(comp, i, merged2)
+            value = early[comp, i] + factor * edges[comp]
             v2[comp, i + 1, rows, :] = value
-            smooth_ref[comp, i] = value
-            packed = pack(3, comp, i, value, packed)
-        return packed
-
-    def sweep_two(i, packed):
-        for comp in range(3):
-            here, flow = flow_of(v1, comp, i, merged2)
-            value = (1.0 - RELAXATION) * here + weight[i] * (2.0 * forc[comp, i] + flow)
-            v2[comp, i + 1, rows, :] = value
-            smooth_ref[comp, i] = value
-            packed = pack(3, comp, i, value, packed)
-        return packed
-
-    waits = ends_first(sweep_two, 3, v2, True, sweep_two_inner)
+            keep_end(3, comp, i, value)
+            yield value
+
+    waits = shell_pass(edges_two, values_two, 3, send_ends(3))
 
     wait_gy()
     for buf, k, count, row in ghost_rows:
@@ -572,30 +612,34 @@
     gz_send[...] = packed
     wait_gz = exchange(14, 2, gz_send, gz_recv.at[0], gz_send, gz_recv.at[1])
 
-    early_flow(v2)
+    def early_misfit(i, carry):
+        for comp in range(3):
+            centre, flow = flow_inner(v2, comp, i)
+            smooth_ref[comp, i] = centre
+            early[comp, i] = flow - diag[i] * centre
+        return carry
+
+    lax.fori_loop(0, cx, early_misfit, 0, unroll=UNROLL)
     for wait in waits:
         wait()
-    late_rows(3, v2)
     merged3 = merged_z(3)
-
-    def misfit_plane(i, total):
+    late_ends(3, False)
+    squares = []
+
+    def edges_three(i):
+        return [edge_of(merged3, comp * cx + i) for comp in range(3)]
+
+    def values_three(i, edges):
+        total = None
         for comp in range(3):
-            here, flow = flow_of(v2, comp, i, merged3)
-            value = forc[comp, i] + 0.5 * (flow - diag[i] * here)
+            value = 0.5 * (early[comp, i] + z_faces[i] * edges[comp])
             misfit_ref[comp, i] = value
-            total = total + value * value
-        return total
-
-    def misfit_inner(i, total):
-        for comp in range(3):
-            value = 0.5 * (late(comp, i, merged3) - diag[i] * v2[comp, i + 1, rows, :])
-            misfit_ref[comp, i] = value
-            total = total + value * value
-        return total
-
-    squares = lax.fori_loop(0, 2, lambda t, carry: misfit_plane(t * (cx - 1), carry), nothing)
-    squares = lax.fori_loop(1, cx - 1, misfit_inner, squares, unroll=UNROLL)
-    part = jnp.sum(squares, axis=0, keepdims=True)
+            total = value * value if total is None else total + value * value
+            yield value
+        squares.append(total if not squares else squares[-1] + total)
+
+    shell_pass(edges_three, values_three, None, None)
+    part = jnp.sum(squares[-1], axis=0, keepdims=True)
 
     def gather(slots, mine, value, peers, sends, recvs):
         slots[mine] = value
@@ -610,10 +654,10 @@
         return copies
 
     def total_of(slots):
-        total = slots[0]
-        for n in range(1, slots.shape[0]):
-            total = total + slots[n]
-        return total
+        parts = [slots[n] for n in range(slots.shape[0])]
+        while len(parts) > 1:
+            parts = [sum(parts[n : n + 2]) for n in range(0, len(parts), 2)]
+        return parts[0]
 
     plane_copies = gather(sums_xy, me_first, part, plane_peers, plane_send, plane_recv)
 
@@ -630,6 +674,8 @@
         size = min(8, height - at)
         target[k, at : at + size, :] = piece[:size, :width]
 
+    for condition, copy in started:
+        pl.when(condition)(copy.wait_send)
     for copy in plane_copies:
         copy.wait()
     whole = total_of(sums_xy)
@@ -641,9 +687,6 @@
     whole = jnp.sum(whole, axis=1, keepdims=True)
     cells_all = float(3 * cx * nx * cy * ny * cz * nz)
     rms_ref[...] = jnp.sqrt(whole / cells_all)
-
-    for condition, copy in started:
-        pl.when(condition)(copy.wait_send)
 
 
 def writer(*refs):
@@ -698,11 +741,15 @@
             pltpu.SMEM(yield_stress.shape, f32),
             v((6, cx, cy, cz), f32),
             v((cx, cy, cz), f32),
+            v((cx, cy, cz), f32),
             v((3, cx, cy, cz), f32),
             v((cx, cy, cz), f32),
             v((cx, cy, cz), f32),
             v((cx // BLOCK, cy, cz), f32),
             v((cx // BLOCK, cy, cz), f32),
+            v((2, 2, 3, cy, cz), f32),
+            v((2, 2, 3, cy, cz), f32),
+            v((2, cy, cz), f32),
             v((4, 2, 3, cx, cz), f32),
             v((4, 2, 3, cx, cz), f32),
             v((4, cy, cz), f32),

time: 32.4 us -> 29.6 us (0.914)
  Pallas kernels: 31.6 us -> 28.8 us
    pallas_call x1, Pallas kernels: 29.7 us -> 26.8 us  [per_device(): pl.pallas_call(functools.partial(kernel, sizes), out_shape=(jax.ShapeDtyp...]
where the time goes in v2:
time: 29.6 us; the launch traced here: 29.4 us
  Pallas kernels  28.8 us (97%)
  between operations  0.64 us (2%)
    pallas_call x1, Pallas kernels, per_device(): pl.pallas_call(functools.partial(kernel, sizes), out_shape=(jax.ShapeDtyp...  26.8 us
    pallas_call x1, Pallas kernels, per_device(): pl.pallas_call(writer, out_shape=tuple((jax.ShapeDtypeStruct(out.shape, f...  1.93 us

profile of v2, /device:TPU:0, one launch (start us, length us, event | category | flops | bytes accessed | tf_op | source)
XLA Modules:
  0.0 29.4 jit_solution(13732291950357256866)
XLA Ops:
  0.6 26.8 %shard_map.117 = (f32[3,16,32,128]{3,2,1,0:T(8,128)S(1)}, f32[16,32,128]{2,1,0:T(8,128)S(1)}, f32[8,16,64]{2,1,0:T(8,128)S(1)}, f32[4,8,32]{2,1,0:T(8,128)S(1)},...) custom-call(f32[3,16,32,128]{3,2,1,0:T(8,128)} %vel_hbm.1, f32[3,16,32,128]{3,2,1,0:T(8,128)} %forc_hbm.1, ...), custom_call_target="tpu_custom_call" | custom-call | tf_op jit(solution)/shard_map/pallas_call | solution.py:719
  27.5 1.9 %shard_map.118 = (f32[3,16,32,128]{3,2,1,0:T(8,128)}, f32[16,32,128]{2,1,0:T(8,128)}, f32[8,16,64]{2,1,0:T(8,128)}, f32[4,8,32]{2,1,0:T(8,128)}, f32[2,4,16]{2,1...) custom-call(f32[3,16,32,128]{3,2,1,0:T(8,128)S(1)} %get-tuple-element.21.refs_0_, ...), custom_call_target="tpu_custom_call" | custom-call | tf_op jit(solution)/shard_map/pallas_call | solution.py:786

commit v3 on v2

--- a/solution.py
+++ b/solution.py
@@ -13,10 +13,8 @@
 PAD = 8
 GHOST = 64
 UNROLL = 4
-VISC_UNROLL = 7
-TILE = 8
-AHEAD = 2
-BEHIND = 2
+STAGES = (2, 0, 2)
+STAGES_VISC = (2, 2, 2)
 ONE_STAGE = 32
 ROUNDS = 4
 MESH = pl.DeviceIdType.MESH
@@ -112,71 +110,85 @@
     local_sem,
     send_sem,
     recv_sem,
-    plane_send,
-    plane_recv,
-    line_send,
-    line_recv,
+    plane_sem,
+    line_sem,
 ):
     nx, ny, nz, cx, cy, cz, phases = sizes
     ix, iy, iz = lax.axis_index("gx"), lax.axis_index("gy"), lax.axis_index("gz")
     rows = pl.ds(PAD, cy)
 
-    vel_in = pltpu.make_async_copy(vel_hbm, v0.at[:, pl.ds(1, cx), rows, :], local_sem.at[0])
-    forc_in = pltpu.make_async_copy(forc_hbm, forc, local_sem.at[1])
-    mats_in = pltpu.make_async_copy(mats_hbm, mats, local_sem.at[2])
-    vel_in.start()
-    phase_in = pltpu.make_async_copy(phase_hbm, phase_ref, local_sem.at[3])
-    phase_in.start()
-    pref_in = pltpu.make_async_copy(pref_hbm, pref_ref, local_sem.at[4])
-    pref_in.start()
-    yield_in = pltpu.make_async_copy(yield_hbm, yield_ref, local_sem.at[5])
-    yield_in.start()
-
-    plane0 = jnp.zeros((3, cy, cz), jnp.float32)
-    for buf in (v0, v1, v2):
-        buf[:, 0, rows, :] = plane0
-        buf[:, cx + 1, rows, :] = plane0
-    row0 = jnp.zeros((3, cx, 1, cz), jnp.float32)
-    visc[1 : cx + 1, PAD - 1 : PAD, :] = row0[0]
-    visc[1 : cx + 1, PAD + cy : PAD + cy + 1, :] = row0[0]
-    for buf in (v1, v2):
-        buf[:, 1 : cx + 1, PAD - 1 : PAD, :] = row0
-        buf[:, 1 : cx + 1, PAD + cy : PAD + cy + 1, :] = row0
-    visc[0, rows, :] = plane0[0]
-    visc[cx + 1, rows, :] = plane0[0]
-    x_recv[...] = jnp.zeros(x_recv.shape, jnp.float32)
-    visc_x[...] = jnp.zeros(visc_x.shape, jnp.float32)
-    y_recv[...] = jnp.zeros(y_recv.shape, jnp.float32)
-    z_recv[...] = jnp.zeros(z_recv.shape, jnp.float32)
-    gx_recv[...] = jnp.zeros(gx_recv.shape, jnp.float32)
-    gy_recv[...] = jnp.zeros(gy_recv.shape, jnp.float32)
-    gz_recv[...] = jnp.zeros(gz_recv.shape, jnp.float32)
+    ends_in = [
+        pltpu.make_async_copy(vel_hbm.at[:, cx - 1], x_send.at[0, 0], local_sem.at[0]),
+        pltpu.make_async_copy(vel_hbm.at[:, 0], x_send.at[0, 1], local_sem.at[1]),
+    ]
+    vel_in = [
+        pltpu.make_async_copy(vel_hbm.at[comp], v0.at[comp, pl.ds(1, cx), rows, :], local_sem.at[2 + comp])
+        for comp in range(3)
+    ]
+    forc_in = pltpu.make_async_copy(forc_hbm, forc, local_sem.at[5])
+    mats_in = pltpu.make_async_copy(mats_hbm, mats, local_sem.at[6])
+    phase_in = pltpu.make_async_copy(phase_hbm, phase_ref, local_sem.at[7])
+    pref_in = pltpu.make_async_copy(pref_hbm, pref_ref, local_sem.at[8])
+    yield_in = pltpu.make_async_copy(yield_hbm, yield_ref, local_sem.at[9])
+    for copy in ends_in + vel_in:
+        copy.start()
 
     barrier = pltpu.get_barrier_semaphore()
+    one_stage = nx * ny * nz <= ONE_STAGE
     me_xy = ix * ny + iy
-    one_stage = nx * ny * nz <= ONE_STAGE
-    plane_peers = []
-    if one_stage:
-        me_first = me_xy * nz + iz
-        for k in range(1, nx * ny * nz):
-            other = lax.rem(me_first + k, nx * ny * nz)
-            plane_peers.append((other // (ny * nz), lax.rem(other // nz, ny), lax.rem(other, nz)))
-        line_peers = []
-    else:
-        me_first = me_xy
-        for k in range(1, nx * ny):
-            other = lax.rem(me_xy + k, nx * ny)
-            plane_peers.append((other // ny, lax.rem(other, ny), iz))
-        line_peers = [(ix, iy, lax.rem(iz + k, nz)) for k in range(1, nz)]
+    me_first = me_xy * nz + iz if one_stage else me_xy
+
+    def first_peers():
+        if one_stage:
+            others = [lax.rem(me_first + k, nx * ny * nz) for k in range(1, nx * ny * nz)]
+            return [(o // (ny * nz), lax.rem(o // nz, ny), lax.rem(o, nz)) for o in others]
+        others = [lax.rem(me_first + k, nx * ny) for k in range(1, nx * ny)]
+        return [(o // ny, lax.rem(o, ny), iz) for o in others]
+
+    line_peers = [] if one_stage else [(ix, iy, lax.rem(iz + k, nz)) for k in range(1, nz)]
     steps = [nx - 1, ny - 1, nz - 1] if one_stage else [nx - 1, ny - 1]
     if sum(steps) - max(steps) <= ROUNDS:
         greeted = [(lax.rem(ix + k, nx), iy, iz) for k in range(1, nx)]
         greeted += [(ix, lax.rem(iy + k, ny), iz) for k in range(1, ny)]
         greeted += [(ix, iy, lax.rem(iz + k, nz)) for k in range(1, nz)]
     else:
-        greeted = plane_peers + line_peers
+        greeted = first_peers() + line_peers
     for peer in greeted:
         pl.semaphore_signal(barrier, inc=1, device_id=peer, device_id_type=MESH)
+    for copy in (phase_in, pref_in, yield_in):
+        copy.start()
+
+    has_up = (ix < nx - 1, iy < ny - 1, iz < nz - 1)
+    has_down = (ix > 0, iy > 0, iz > 0)
+
+    def clear(ref):
+        ref[...] = jnp.zeros(ref.shape, jnp.float32)
+
+    for side, present in ((0, has_down), (1, has_up)):
+        @pl.when(jnp.logical_not(present[0]))
+        def _():
+            for r in range(3):
+                clear(x_recv.at[r, side])
+            clear(visc_x.at[side])
+            clear(gx_recv.at[side])
+
+        @pl.when(jnp.logical_not(present[1]))
+        def _():
+            for r in range(4):
+                clear(y_recv.at[r, side])
+            clear(gy_recv.at[side])
+
+        @pl.when(jnp.logical_not(present[2]))
+        def _():
+            for r in range(4):
+                clear(z_recv.at[r, side])
+            clear(gz_recv.at[side])
+
+    for buf in [v.at[comp] for v in (v0, v1, v2) for comp in range(3)] + [visc]:
+        clear(buf.at[0, rows])
+        clear(buf.at[cx + 1, rows])
+        clear(buf.at[pl.ds(1, cx), pl.ds(PAD - 1, 1)])
+        clear(buf.at[pl.ds(1, cx), pl.ds(PAD + cy, 1)])
 
     lane = lax.broadcasted_iota(jnp.int32, (cy, cz), 1)
     odd_lane = lax.rem(lane, 2) == 1
@@ -195,8 +207,6 @@
         (ix, lax.rem(iy + ny - 1, ny), iz),
         (ix, iy, lax.rem(iz + nz - 1, nz)),
     )
-    has_up = (ix < nx - 1, iy < ny - 1, iz < nz - 1)
-    has_down = (ix > 0, iy > 0, iz > 0)
     started = []
 
     def exchange(slot, dim, up_src, up_dst, down_src, down_dst):
@@ -266,18 +276,20 @@
         ym, yp, zm, zp = along(buf.at[comp, i + 1], centre, merged, comp * cx + i)
         return centre, (buf[comp, i, rows, :], buf[comp, i + 2, rows, :], ym, yp, zm, zp)
 
-    vel_in.wait()
+    for copy in ends_in:
+        copy.wait()
+    pl.semaphore_wait(barrier, len(greeted))
+    waits = [send_x(0, x_send.at[0, 0], x_recv.at[0, 0], x_send.at[0, 1], x_recv.at[0, 1])]
+    nothing = jnp.zeros((cy, cz), jnp.float32)
+    packed = nothing
+    for comp in range(3):
+        vel_in[comp].wait()
+        for i in range(cx):
+            packed = pack(0, comp, i, v0[comp, i + 1, rows, :], packed)
+    z_send[0] = packed
+    waits += send_yz(0)
     forc_in.start()
     mats_in.start()
-
-    nothing = jnp.zeros((cy, cz), jnp.float32)
-    packed = nothing
-    for i in range(cx):
-        for comp in range(3):
-            packed = pack(0, comp, i, v0[comp, i + 1, rows, :], packed)
-    z_send[0] = packed
-    pl.semaphore_wait(barrier, len(greeted))
-    waits = [send_x(0, v0.at[:, cx, rows, :], v0.at[:, 0, rows, :], v0.at[:, 1, rows, :], v0.at[:, cx + 1, rows, :])] + send_yz(0)
 
     phase_in.wait()
     pref_in.wait()
@@ -308,34 +320,69 @@
     for buf in (t1, t2a, t2b, t3a, t3b, t3c):
         buf[...] = jnp.zeros(buf.shape, jnp.float32)
 
+    along_x, along_y, along_z = (0, 3, 4), (3, 1, 5), (4, 5, 2)
+
+    def early_strain(i, carry):
+        found = {}
+        for comp in range(3):
+            plane = v0.at[comp, i + 1]
+            centre = plane[rows, :]
+            low = jnp.where(first_lane, 0.0, pltpu.roll(centre, 1, 1))
+            high = jnp.where(last_lane, 0.0, pltpu.roll(centre, cz - 1, 1))
+            for n, jump in (
+                (along_x[comp], v0[comp, i + 2, rows, :] - v0[comp, i, rows, :]),
+                (along_y[comp], plane[PAD + 1 : PAD + 1 + cy, :] - plane[PAD - 1 : PAD - 1 + cy, :]),
+                (along_z[comp], high - low),
+            ):
+                found[n] = found[n] + jump if n in found else jump
+        for n in range(6):
+            faces[n, i] = found[n]
+        return carry
+
+    lax.fori_loop(0, cx, early_strain, 0, unroll=UNROLL)
     for wait in waits:
         wait()
-    unpack_y(0, v0, 3)
     merged0 = merged_z(0)
+    signed0 = jnp.where(odd_lane, -merged0, merged0)
+    for comp in range(3):
+        n = along_x[comp]
+        faces[n, 0] = faces[n, 0] - x_recv[0, 0, comp]
+        faces[n, cx - 1] = faces[n, cx - 1] + x_recv[0, 1, comp]
+
+    def late_strain(i, carry):
+        for comp in range(3):
+            n = along_y[comp]
+            faces[n, i, 0:1, :] = faces[n, i, 0:1, :] - y_recv[0, 0, comp, pl.ds(i, 1), :]
+            faces[n, i, cy - 1 : cy, :] = faces[n, i, cy - 1 : cy, :] + y_recv[0, 1, comp, pl.ds(i, 1), :]
+        return carry
+
+    lax.fori_loop(0, cx, late_strain, 0, unroll=UNROLL)
 
     order = [0, cx - 1] + list(range(1, cx - 1))
 
-    def shell_pass(edge, value_of, r, send_ends, vector=True):
-        comps = 3 if vector else 1
+    def shell_pass(edge, value_of, r, send_ends, stages):
+        ahead, hold, behind = stages
         packed = nothing
-        edges, rolled = {}, {}
+        edges, values, rolled = {}, {}, {}
         sent = None
-        for t in range(cx + AHEAD + BEHIND):
+        for t in range(cx + ahead + hold + behind):
             if t < cx:
                 edges[t] = edge(order[t])
-            n = t - AHEAD
+            n = t - ahead
             if 0 <= n < cx:
                 i = order[n]
-                moved = []
+                values[n] = []
                 for comp, value in enumerate(value_of(i, edges.pop(n))):
                     if r is not None:
                         y_send[r, 0, comp, pl.ds(i, 1), :] = value[cy - 1 : cy, :]
                         y_send[r, 1, comp, pl.ds(i, 1), :] = value[0:1, :]
-                        moved.append((comp * cx + i, pltpu.roll(value, 2 * (comp * cx + i) + 2, 1)))
-                rolled[n] = moved
+                        values[n].append((comp * cx + i, value))
                 if n == 1 and send_ends is not None:
                     sent = send_ends()
-            n = t - AHEAD - BEHIND
+            n = t - ahead - hold
+            if 0 <= n < cx:
+                rolled[n] = [(place, pltpu.roll(value, 2 * place + 2, 1)) for place, value in values.pop(n)]
+            n = t - ahead - hold - behind
             if 0 <= n < cx:
                 for place, value in rolled.pop(n):
                     packed = jnp.where(lane_pair == place, value, packed)
@@ -347,45 +394,32 @@
     def edge_of(merged, place):
         return pltpu.roll(merged, cz - 1 - 2 * place, 1)
 
-    def visc_plane(i, carry):
-        packed, held, at = carry
-        out = []
-        centres = [v0[comp, i + 1, rows, :] for comp in range(3)]
-        edges = [edge_of(merged0, comp * cx + i) for comp in range(3)]
-        lows = [pltpu.roll(centre, 1, 1) for centre in centres]
-        highs = [pltpu.roll(centre, cz - 1, 1) for centre in centres]
-        moved = pltpu.roll(held, 2 * at + 2, 1)
-        packed = jnp.where(lane_pair == at, moved, packed)
-        jump = []
-        for comp in range(3):
-            plane = v0.at[comp, i + 1]
-            below = jnp.where(first_lane, edges[comp], lows[comp])
-            above = jnp.where(last_lane, edges[comp], highs[comp])
-            jump.append((
-                v0[comp, i + 2, rows, :] - v0[comp, i, rows, :],
-                plane[PAD + 1 : PAD + 1 + cy, :] - plane[PAD - 1 : PAD - 1 + cy, :],
-                above - below,
-            ))
-        straight = sum(jump[a][a] * jump[a][a] for a in range(3))
-        skew = None
-        for a, b in ((0, 1), (0, 2), (1, 2)):
-            both = jump[a][b] + jump[b][a]
-            skew = both * both if skew is None else skew + both * both
+    def edges_visc(i):
+        return [edge_of(signed0, comp * cx + i) for comp in range(3)]
+
+    def values_visc(i, edges):
+        strain = [faces[n, i] for n in range(6)]
+        for comp in range(3):
+            n = along_z[comp]
+            strain[n] = strain[n] + jnp.where(end_lane, edges[comp], 0.0)
+        squared = [term * term for term in strain]
+        straight = squared[0] + squared[1] + squared[2]
+        skew = squared[3] + squared[4] + squared[5]
         invariant = 1.0 + (0.125 * straight + 0.0625 * skew)
         creeping = pref_cells[i // BLOCK] * jnp.exp(jnp.log(invariant) * (-1.0 / 3.0))
         plastic = yield_cells[i // BLOCK] * lax.rsqrt(invariant)
         value = jnp.minimum(creeping, plastic)
         visc[i + 1, rows, :] = value
-        visc_ref[i] = value
-        y_send[1, 0, 0, pl.ds(i, 1), :] = value[cy - 1 : cy, :]
-        y_send[1, 1, 0, pl.ds(i, 1), :] = value[0:1, :]
-        return packed, value, i
-
-    carry = visc_plane(cx - 1, visc_plane(0, (nothing, nothing, 0)))
-    sent = send_x(1, visc.at[cx, rows, :], visc_x.at[0], visc.at[1, rows, :], visc_x.at[1])
-    packed, held, at = lax.fori_loop(1, cx - 1, visc_plane, carry, unroll=VISC_UNROLL)
-    z_send[1] = jnp.where(lane_pair == at, pltpu.roll(held, 2 * at + 2, 1), packed)
-    waits = [sent] + send_yz(1)
+        yield value
+
+    def send_visc():
+        return send_x(1, visc.at[cx, rows, :], visc_x.at[0], visc.at[1, rows, :], visc_x.at[1])
+
+    waits = shell_pass(edges_visc, values_visc, 1, send_visc, STAGES_VISC)
+    for comp in range(3):
+        v0[comp, 0, rows, :] = x_recv[0, 0, comp]
+        v0[comp, cx + 1, rows, :] = x_recv[0, 1, comp]
+    unpack_y(0, v0, 3)
 
     def flag(condition):
         return jnp.where(condition, 1.0, 0.0).astype(jnp.float32)
@@ -416,6 +450,7 @@
     def early_one(i, carry):
         plane = visc.at[i + 1]
         centre = plane[rows, :]
+        visc_ref[i] = centre
         sides = (
             centre + visc[i, rows, :],
             centre + visc[i + 2, rows, :],
@@ -480,16 +515,16 @@
             yield value
 
     def send_ends(r):
-        s = r - 2
+        s = r - 1
         return lambda: send_x(r, x_send.at[s, 0], x_recv.at[s, 0], x_send.at[s, 1], x_recv.at[s, 1])
 
     def keep_end(r, comp, i, value):
         if i == cx - 1:
-            x_send[r - 2, 0, comp] = value
+            x_send[r - 1, 0, comp] = value
         if i == 0:
-            x_send[r - 2, 1, comp] = value
-
-    waits = shell_pass(edges_one, values_one, 2, send_ends(2))
+            x_send[r - 1, 1, comp] = value
+
+    waits = shell_pass(edges_one, values_one, 2, send_ends(2), STAGES)
 
     wait_gx()
     low_y, high_y = flag(has_down[1]), flag(has_up[1])
@@ -553,7 +588,7 @@
             if scaled:
                 factor = factor * weight[i]
             for comp in range(3):
-                early[comp, i] = early[comp, i] + factor * x_recv[r - 2, side, comp]
+                early[comp, i] = early[comp, i] + factor * x_recv[r - 1, side, comp]
 
         def body(i, carry):
             for side, face, at in ((0, 2, 0), (1, 3, cy - 1)):
@@ -584,7 +619,7 @@
             keep_end(3, comp, i, value)
             yield value
 
-    waits = shell_pass(edges_two, values_two, 3, send_ends(3))
+    waits = shell_pass(edges_two, values_two, 3, send_ends(3), STAGES)
 
     wait_gy()
     for buf, k, count, row in ghost_rows:
@@ -638,20 +673,20 @@
             yield value
         squares.append(total if not squares else squares[-1] + total)
 
-    shell_pass(edges_three, values_three, None, None)
+    shell_pass(edges_three, values_three, None, None, STAGES)
     part = jnp.sum(squares[-1], axis=0, keepdims=True)
 
-    def gather(slots, mine, value, peers, sends, recvs):
+    def gather(slots, mine, value, peers, sems):
         slots[mine] = value
-        copies = []
-        for k, peer in enumerate(peers):
-            copy = pltpu.make_async_remote_copy(
-                slots.at[mine], slots.at[mine], sends.at[k], recvs.at[k],
+        for peer in peers:
+            pltpu.make_async_remote_copy(
+                slots.at[mine], slots.at[mine], sems.at[0], sems.at[1],
                 device_id=peer, device_id_type=MESH,
-            )
-            copy.start()
-            copies.append(copy)
-        return copies
+            ).start()
+        others = slots.at[pl.ds(0, len(peers))]
+        return pltpu.make_async_remote_copy(
+            others, others, sems.at[0], sems.at[1], device_id=peers[0], device_id_type=MESH
+        )
 
     def total_of(slots):
         parts = [slots[n] for n in range(slots.shape[0])]
@@ -659,7 +694,7 @@
             parts = [sum(parts[n : n + 2]) for n in range(0, len(parts), 2)]
         return parts[0]
 
-    plane_copies = gather(sums_xy, me_first, part, plane_peers, plane_send, plane_recv)
+    plane_copies = gather(sums_xy, me_first, part, first_peers(), plane_sem)
 
     wait_gz()
     low_part, high_part = gz_recv[0], gz_recv[1]
@@ -676,13 +711,10 @@
 
     for condition, copy in started:
         pl.when(condition)(copy.wait_send)
-    for copy in plane_copies:
-        copy.wait()
+    plane_copies.wait()
     whole = total_of(sums_xy)
     if not one_stage:
-        line_copies = gather(sums_z, iz, whole, line_peers, line_send, line_recv)
-        for copy in line_copies:
-            copy.wait()
+        gather(sums_z, iz, whole, line_peers, line_sem).wait()
         whole = total_of(sums_z)
     whole = jnp.sum(whole, axis=1, keepdims=True)
     cells_all = float(3 * cx * nx * cy * ny * cz * nz)
@@ -747,8 +779,8 @@
             v((cx, cy, cz), f32),
             v((cx // BLOCK, cy, cz), f32),
             v((cx // BLOCK, cy, cz), f32),
-            v((2, 2, 3, cy, cz), f32),
-            v((2, 2, 3, cy, cz), f32),
+            v((3, 2, 3, cy, cz), f32),
+            v((3, 2, 3, cy, cz), f32),
             v((2, cy, cz), f32),
             v((4, 2, 3, cx, cz), f32),
             v((4, 2, 3, cx, cz), f32),
@@ -771,13 +803,11 @@
             v((2, 8, cz), f32),
             v((firsts, 1, cz), f32),
             v((nz, 1, cz), f32),
-            dma((6,)),
+            dma((10,)),
             dma((15, 2)),
             dma((15, 2)),
-            dma((firsts - 1,)),
-            dma((firsts - 1,)),
-            dma((nz - 1,)),
-            dma((nz - 1,)),
+            dma((2,)),
+            dma((2,)),
         ],
         compiler_params=pltpu.CompilerParams(
             collective_id=0, has_side_effects=True, vmem_limit_bytes=40 * 1024 * 1024

time: 29.6 us -> 28.1 us (0.949)
  Pallas kernels: 28.8 us -> 27.3 us
    pallas_call x1, Pallas kernels: 26.8 us -> 25.3 us  [per_device(): pl.pallas_call(functools.partial(kernel, sizes), out_shape=(jax.ShapeDtyp...]
where the time goes in v3:
time: 28.1 us; the launch traced here: 27.9 us
  Pallas kernels  27.3 us (97%)
  between operations  0.64 us (2%)
    pallas_call x1, Pallas kernels, per_device(): pl.pallas_call(functools.partial(kernel, sizes), out_shape=(jax.ShapeDtyp...  25.3 us
    pallas_call x1, Pallas kernels, per_device(): pl.pallas_call(writer, out_shape=tuple((jax.ShapeDtypeStruct(out.shape, f...  1.93 us

profile of v3, /device:TPU:0, one launch (start us, length us, event | category | flops | bytes accessed | tf_op | source)
XLA Modules:
  0.0 27.9 jit_solution(18108735616241213023)
XLA Ops:
  0.6 25.3 %shard_map.117 = (f32[3,16,32,128]{3,2,1,0:T(8,128)S(1)}, f32[16,32,128]{2,1,0:T(8,128)S(1)}, f32[8,16,64]{2,1,0:T(8,128)S(1)}, f32[4,8,32]{2,1,0:T(8,128)S(1)},...) custom-call(f32[3,16,32,128]{3,2,1,0:T(8,128)} %vel_hbm.1, f32[3,16,32,128]{3,2,1,0:T(8,128)} %forc_hbm.1, ...), custom_call_target="tpu_custom_call" | custom-call | tf_op jit(solution)/shard_map/pallas_call | solution.py:751
  26.0 1.9 %shard_map.118 = (f32[3,16,32,128]{3,2,1,0:T(8,128)}, f32[16,32,128]{2,1,0:T(8,128)}, f32[8,16,64]{2,1,0:T(8,128)}, f32[4,8,32]{2,1,0:T(8,128)}, f32[2,4,16]{2,1...) custom-call(f32[3,16,32,128]{3,2,1,0:T(8,128)S(1)} %get-tuple-element.21.refs_0_, ...), custom_call_target="tpu_custom_call" | custom-call | tf_op jit(solution)/shard_map/pallas_call | solution.py:816

commit v4 on v3

--- a/solution.py
+++ b/solution.py
@@ -13,7 +13,7 @@
 PAD = 8
 GHOST = 64
 UNROLL = 4
-STAGES = (2, 0, 2)
+STAGES = (3, 0, 1)
 STAGES_VISC = (2, 2, 2)
 ONE_STAGE = 32
 ROUNDS = 4
@@ -112,6 +112,7 @@
     recv_sem,
     plane_sem,
     line_sem,
+    hello_sem,
 ):
     nx, ny, nz, cx, cy, cz, phases = sizes
     ix, iy, iz = lax.axis_index("gx"), lax.axis_index("gy"), lax.axis_index("gz")
@@ -146,57 +147,8 @@
         return [(o // ny, lax.rem(o, ny), iz) for o in others]
 
     line_peers = [] if one_stage else [(ix, iy, lax.rem(iz + k, nz)) for k in range(1, nz)]
-    steps = [nx - 1, ny - 1, nz - 1] if one_stage else [nx - 1, ny - 1]
-    if sum(steps) - max(steps) <= ROUNDS:
-        greeted = [(lax.rem(ix + k, nx), iy, iz) for k in range(1, nx)]
-        greeted += [(ix, lax.rem(iy + k, ny), iz) for k in range(1, ny)]
-        greeted += [(ix, iy, lax.rem(iz + k, nz)) for k in range(1, nz)]
-    else:
-        greeted = first_peers() + line_peers
-    for peer in greeted:
-        pl.semaphore_signal(barrier, inc=1, device_id=peer, device_id_type=MESH)
-    for copy in (phase_in, pref_in, yield_in):
-        copy.start()
-
     has_up = (ix < nx - 1, iy < ny - 1, iz < nz - 1)
     has_down = (ix > 0, iy > 0, iz > 0)
-
-    def clear(ref):
-        ref[...] = jnp.zeros(ref.shape, jnp.float32)
-
-    for side, present in ((0, has_down), (1, has_up)):
-        @pl.when(jnp.logical_not(present[0]))
-        def _():
-            for r in range(3):
-                clear(x_recv.at[r, side])
-            clear(visc_x.at[side])
-            clear(gx_recv.at[side])
-
-        @pl.when(jnp.logical_not(present[1]))
-        def _():
-            for r in range(4):
-                clear(y_recv.at[r, side])
-            clear(gy_recv.at[side])
-
-        @pl.when(jnp.logical_not(present[2]))
-        def _():
-            for r in range(4):
-                clear(z_recv.at[r, side])
-            clear(gz_recv.at[side])
-
-    for buf in [v.at[comp] for v in (v0, v1, v2) for comp in range(3)] + [visc]:
-        clear(buf.at[0, rows])
-        clear(buf.at[cx + 1, rows])
-        clear(buf.at[pl.ds(1, cx), pl.ds(PAD - 1, 1)])
-        clear(buf.at[pl.ds(1, cx), pl.ds(PAD + cy, 1)])
-
-    lane = lax.broadcasted_iota(jnp.int32, (cy, cz), 1)
-    odd_lane = lax.rem(lane, 2) == 1
-    lane_pair = (lane - 1) // 2
-    first_lane = lane == 0
-    last_lane = lane == cz - 1
-    end_lane = first_lane | last_lane
-
     up_ids = (
         (lax.rem(ix + 1, nx), iy, iz),
         (ix, lax.rem(iy + 1, ny), iz),
@@ -207,6 +159,66 @@
         (ix, lax.rem(iy + ny - 1, ny), iz),
         (ix, iy, lax.rem(iz + nz - 1, nz)),
     )
+    z_line = [(ix, iy, lax.rem(iz + k, nz)) for k in range(1, nz)]
+    steps = [nx - 1, ny - 1, nz - 1] if one_stage else [nx - 1, ny - 1]
+    near_only = one_stage and steps[0] + steps[1] <= ROUNDS and steps[2] <= ROUNDS
+    if near_only:
+        met = 0
+        for there, peer in list(zip(has_up, up_ids)) + list(zip(has_down, down_ids)):
+            met = met + there.astype(jnp.int32)
+
+            @pl.when(there)
+            def _():
+                pl.semaphore_signal(barrier, inc=1, device_id=peer, device_id_type=MESH)
+    else:
+        if sum(steps) - max(steps) <= ROUNDS:
+            greeted = [(lax.rem(ix + k, nx), iy, iz) for k in range(1, nx)]
+            greeted += [(ix, lax.rem(iy + k, ny), iz) for k in range(1, ny)]
+            greeted += z_line
+        else:
+            greeted = first_peers() + line_peers
+        met = len(greeted)
+        for peer in greeted:
+            pl.semaphore_signal(barrier, inc=1, device_id=peer, device_id_type=MESH)
+    for copy in (phase_in, pref_in, yield_in):
+        copy.start()
+
+    def clear(ref):
+        ref[...] = jnp.zeros(ref.shape, jnp.float32)
+
+    for side, present in ((0, has_down), (1, has_up)):
+        @pl.when(jnp.logical_not(present[0]))
+        def _():
+            for r in range(3):
+                clear(x_recv.at[r, side])
+            clear(visc_x.at[side])
+            clear(gx_recv.at[side])
+
+        @pl.when(jnp.logical_not(present[1]))
+        def _():
+            for r in range(4):
+                clear(y_recv.at[r, side])
+            clear(gy_recv.at[side])
+
+        @pl.when(jnp.logical_not(present[2]))
+        def _():
+            for r in range(4):
+                clear(z_recv.at[r, side])
+            clear(gz_recv.at[side])
+
+    for buf in [v.at[comp] for v in (v0, v1, v2) for comp in range(3)] + [visc]:
+        clear(buf.at[0, rows])
+        clear(buf.at[cx + 1, rows])
+        clear(buf.at[pl.ds(1, cx), pl.ds(PAD - 1, 1)])
+        clear(buf.at[pl.ds(1, cx), pl.ds(PAD + cy, 1)])
+
+    lane = lax.broadcasted_iota(jnp.int32, (cy, cz), 1)
+    odd_lane = lax.rem(lane, 2) == 1
+    lane_pair = (lane - 1) // 2
+    first_lane = lane == 0
+    last_lane = lane == cz - 1
+    end_lane = first_lane | last_lane
+
     started = []
 
     def exchange(slot, dim, up_src, up_dst, down_src, down_dst):
@@ -278,7 +290,7 @@
 
     for copy in ends_in:
         copy.wait()
-    pl.semaphore_wait(barrier, len(greeted))
+    pl.semaphore_wait(barrier, met)
     waits = [send_x(0, x_send.at[0, 0], x_recv.at[0, 0], x_send.at[0, 1], x_recv.at[0, 1])]
     nothing = jnp.zeros((cy, cz), jnp.float32)
     packed = nothing
@@ -349,18 +361,15 @@
         faces[n, 0] = faces[n, 0] - x_recv[0, 0, comp]
         faces[n, cx - 1] = faces[n, cx - 1] + x_recv[0, 1, comp]
 
-    def late_strain(i, carry):
+    def late_strain(i):
         for comp in range(3):
             n = along_y[comp]
             faces[n, i, 0:1, :] = faces[n, i, 0:1, :] - y_recv[0, 0, comp, pl.ds(i, 1), :]
             faces[n, i, cy - 1 : cy, :] = faces[n, i, cy - 1 : cy, :] + y_recv[0, 1, comp, pl.ds(i, 1), :]
-        return carry
-
-    lax.fori_loop(0, cx, late_strain, 0, unroll=UNROLL)
 
     order = [0, cx - 1] + list(range(1, cx - 1))
 
-    def shell_pass(edge, value_of, r, send_ends, stages):
+    def shell_pass(fix, edge, value_of, r, send_ends, stages):
         ahead, hold, behind = stages
         packed = nothing
         edges, values, rolled = {}, {}, {}
@@ -368,6 +377,7 @@
         for t in range(cx + ahead + hold + behind):
             if t < cx:
                 edges[t] = edge(order[t])
+                fix(order[t])
             n = t - ahead
             if 0 <= n < cx:
                 i = order[n]
@@ -415,7 +425,7 @@
     def send_visc():
         return send_x(1, visc.at[cx, rows, :], visc_x.at[0], visc.at[1, rows, :], visc_x.at[1])
 
-    waits = shell_pass(edges_visc, values_visc, 1, send_visc, STAGES_VISC)
+    waits = shell_pass(late_strain, edges_visc, values_visc, 1, send_visc, STAGES_VISC)
     for comp in range(3):
         v0[comp, 0, rows, :] = x_recv[0, 0, comp]
         v0[comp, cx + 1, rows, :] = x_recv[0, 1, comp]
@@ -484,7 +494,7 @@
         for comp in range(3):
             early[comp, i] = early[comp, i] + halo * v0[comp, halo_plane, rows, :]
 
-    def late_one(i, carry):
+    def late_one(i):
         ends = ((0, 2, 0, PAD - 1), (1, 3, cy - 1, PAD + cy))
         for side, face, at, row in ends:
             halo = y_recv[1, side, 0, pl.ds(i, 1), :]
@@ -493,9 +503,6 @@
             for comp in range(3):
                 near = v0[comp, i + 1, row : row + 1, :]
                 early[comp, i, at : at + 1, :] = early[comp, i, at : at + 1, :] + halo * near
-        return carry
-
-    lax.fori_loop(0, cx, late_one, 0, unroll=UNROLL)
 
     def edges_one(i):
         return [edge_of(merged1, i)] + [edge_of(merged0, comp * cx + i) for comp in range(3)]
@@ -524,7 +531,7 @@
         if i == 0:
             x_send[r - 1, 1, comp] = value
 
-    waits = shell_pass(edges_one, values_one, 2, send_ends(2), STAGES)
+    waits = shell_pass(late_one, edges_one, values_one, 2, send_ends(2), STAGES)
 
     wait_gx()
     low_y, high_y = flag(has_down[1]), flag(has_up[1])
@@ -582,7 +589,7 @@
             early[comp, i] = (1.0 - RELAXATION) * centre + weight[i] * flow
         return carry
 
-    def late_ends(r, scaled):
+    def late_planes(r, scaled):
         for side, i, face in ((0, 0, 0), (1, cx - 1, 1)):
             factor = faces[face, i]
             if scaled:
@@ -590,7 +597,8 @@
             for comp in range(3):
                 early[comp, i] = early[comp, i] + factor * x_recv[r - 1, side, comp]
 
-        def body(i, carry):
+    def late_rows(r, scaled):
+        def fix(i):
             for side, face, at in ((0, 2, 0), (1, 3, cy - 1)):
                 factor = faces[face, i, at : at + 1, :]
                 if scaled:
@@ -598,15 +606,14 @@
                 for comp in range(3):
                     halo = y_recv[r, side, comp, pl.ds(i, 1), :]
                     early[comp, i, at : at + 1, :] = early[comp, i, at : at + 1, :] + factor * halo
-            return carry
-
-        lax.fori_loop(0, cx, body, 0, unroll=UNROLL)
+
+        return fix
 
     lax.fori_loop(0, cx, early_two, 0, unroll=UNROLL)
     for wait in waits:
         wait()
     merged2 = merged_z(2)
-    late_ends(2, True)
+    late_planes(2, True)
 
     def edges_two(i):
         return [edge_of(merged2, comp * cx + i) for comp in range(3)]
@@ -619,7 +626,7 @@
             keep_end(3, comp, i, value)
             yield value
 
-    waits = shell_pass(edges_two, values_two, 3, send_ends(3), STAGES)
+    waits = shell_pass(late_rows(2, True), edges_two, values_two, 3, send_ends(3), STAGES)
 
     wait_gy()
     for buf, k, count, row in ghost_rows:
@@ -654,11 +661,14 @@
             early[comp, i] = flow - diag[i] * centre
         return carry
 
+    if near_only:
+        for peer in z_line:
+            pl.semaphore_signal(hello_sem, inc=1, device_id=peer, device_id_type=MESH)
     lax.fori_loop(0, cx, early_misfit, 0, unroll=UNROLL)
     for wait in waits:
         wait()
     merged3 = merged_z(3)
-    late_ends(3, False)
+    late_planes(3, False)
     squares = []
 
     def edges_three(i):
@@ -673,7 +683,7 @@
             yield value
         squares.append(total if not squares else squares[-1] + total)
 
-    shell_pass(edges_three, values_three, None, None, STAGES)
+    shell_pass(late_rows(3, False), edges_three, values_three, None, None, STAGES)
     part = jnp.sum(squares[-1], axis=0, keepdims=True)
 
     def gather(slots, mine, value, peers, sems):
@@ -694,6 +704,8 @@
             parts = [sum(parts[n : n + 2]) for n in range(0, len(parts), 2)]
         return parts[0]
 
+    if near_only:
+        pl.semaphore_wait(hello_sem, nz - 1)
     plane_copies = gather(sums_xy, me_first, part, first_peers(), plane_sem)
 
     wait_gz()
@@ -808,6 +820,7 @@
             dma((15, 2)),
             dma((2,)),
             dma((2,)),
+            pltpu.SemaphoreType.REGULAR,
         ],
         compiler_params=pltpu.CompilerParams(
             collective_id=0, has_side_effects=True, vmem_limit_bytes=40 * 1024 * 1024

time: 28.1 us -> 27.1 us (0.964)
  Pallas kernels: 27.3 us -> 26.3 us
    pallas_call x1, Pallas kernels: 25.3 us -> 24.4 us  [per_device(): pl.pallas_call(functools.partial(kernel, sizes), out_shape=(jax.ShapeDtyp...]
where the time goes in v4:
time: 27.1 us; the launch traced here: 27 us
  Pallas kernels  26.3 us (97%)
  between operations  0.64 us (2%)
    pallas_call x1, Pallas kernels, per_device(): pl.pallas_call(functools.partial(kernel, sizes), out_shape=(jax.ShapeDtyp...  24.4 us
    pallas_call x1, Pallas kernels, per_device(): pl.pallas_call(writer, out_shape=tuple((jax.ShapeDtypeStruct(out.shape, f...  1.93 us

profile of v4, /device:TPU:0, one launch (start us, length us, event | category | flops | bytes accessed | tf_op | source)
XLA Modules:
  0.0 27.0 jit_solution(3292457142319172897)
XLA Ops:
  0.6 24.4 %shard_map.117 = (f32[3,16,32,128]{3,2,1,0:T(8,128)S(1)}, f32[16,32,128]{2,1,0:T(8,128)S(1)}, f32[8,16,64]{2,1,0:T(8,128)S(1)}, f32[4,8,32]{2,1,0:T(8,128)S(1)},...) custom-call(f32[3,16,32,128]{3,2,1,0:T(8,128)} %vel_hbm.1, f32[3,16,32,128]{3,2,1,0:T(8,128)} %forc_hbm.1, ...), custom_call_target="tpu_custom_call" | custom-call | tf_op jit(solution)/shard_map/pallas_call | solution.py:763
  25.0 1.9 %shard_map.118 = (f32[3,16,32,128]{3,2,1,0:T(8,128)}, f32[16,32,128]{2,1,0:T(8,128)}, f32[8,16,64]{2,1,0:T(8,128)}, f32[4,8,32]{2,1,0:T(8,128)}, f32[2,4,16]{2,1...) custom-call(f32[3,16,32,128]{3,2,1,0:T(8,128)S(1)} %get-tuple-element.21.refs_0_, ...), custom_call_target="tpu_custom_call" | custom-call | tf_op jit(solution)/shard_map/pallas_call | solution.py:829

commit v5 on v4

--- a/solution.py
+++ b/solution.py
@@ -78,6 +78,7 @@
     faces,
     z_faces,
     z_scaled,
+    edge0,
     early,
     weight,
     diag,
@@ -271,22 +272,9 @@
 
         lax.fori_loop(0, cx, body, 0)
 
-    def merged_z(r):
-        return jnp.where(odd_lane, z_recv[r, 0], pltpu.roll(z_recv[r, 1], cz - 2, 1))
-
-    def along(plane_ref, centre, merged, place):
-        edge = pltpu.roll(merged, cz - 1 - 2 * place, 1)
-        return (
-            plane_ref[PAD - 1 : PAD - 1 + cy, :],
-            plane_ref[PAD + 1 : PAD + 1 + cy, :],
-            jnp.where(first_lane, edge, pltpu.roll(centre, 1, 1)),
-            jnp.where(last_lane, edge, pltpu.roll(centre, cz - 1, 1)),
-        )
-
-    def around(buf, comp, i, merged):
-        centre = buf[comp, i + 1, rows, :]
-        ym, yp, zm, zp = along(buf.at[comp, i + 1], centre, merged, comp * cx + i)
-        return centre, (buf[comp, i, rows, :], buf[comp, i + 2, rows, :], ym, yp, zm, zp)
+    def halos_z(r):
+        low, high = z_recv[r, 0], z_recv[r, 1]
+        return jnp.where(odd_lane, low, high), jnp.where(odd_lane, low, pltpu.roll(high, cz - 2, 1))
 
     for copy in ends_in:
         copy.wait()
@@ -294,8 +282,9 @@
     waits = [send_x(0, x_send.at[0, 0], x_recv.at[0, 0], x_send.at[0, 1], x_recv.at[0, 1])]
     nothing = jnp.zeros((cy, cz), jnp.float32)
     packed = nothing
+    for copy in vel_in:
+        copy.wait()
     for comp in range(3):
-        vel_in[comp].wait()
         for i in range(cx):
             packed = pack(0, comp, i, v0[comp, i + 1, rows, :], packed)
     z_send[0] = packed
@@ -354,8 +343,9 @@
     lax.fori_loop(0, cx, early_strain, 0, unroll=UNROLL)
     for wait in waits:
         wait()
-    merged0 = merged_z(0)
-    signed0 = jnp.where(odd_lane, -merged0, merged0)
+    halos0 = halos_z(0)
+    merged0 = halos0[1]
+    signed0 = [jnp.where(odd_lane, -halo, halo) for halo in halos0]
     for comp in range(3):
         n = along_x[comp]
         faces[n, 0] = faces[n, 0] - x_recv[0, 0, comp]
@@ -404,8 +394,14 @@
     def edge_of(merged, place):
         return pltpu.roll(merged, cz - 1 - 2 * place, 1)
 
+    def edge_at(halos, i, place):
+        mixed, merged = halos
+        if i in (0, cx - 1):
+            return jnp.where(first_lane, edge_of(mixed, place), edge_of(mixed, place + 1))
+        return edge_of(merged, place)
+
     def edges_visc(i):
-        return [edge_of(signed0, comp * cx + i) for comp in range(3)]
+        return [edge_at(signed0, i, comp * cx + i) for comp in range(3)]
 
     def values_visc(i, edges):
         strain = [faces[n, i] for n in range(6)]
@@ -475,7 +471,18 @@
         faces[5, i] = jnp.where(last_lane, 0.0, sides[5])
         diag[i] = (sides[0] + sides[1]) + (sides[2] + sides[3]) + (sides[4] + sides[5])
         for comp in range(3):
-            _, near = around(v0, comp, i, merged0)
+            plane = v0.at[comp, i + 1]
+            centre = plane[rows, :]
+            edge = edge_of(merged0, comp * cx + i)
+            edge0[comp, i] = edge
+            near = (
+                v0[comp, i, rows, :],
+                v0[comp, i + 2, rows, :],
+                plane[PAD - 1 : PAD - 1 + cy, :],
+                plane[PAD + 1 : PAD + 1 + cy, :],
+                jnp.where(first_lane, edge, pltpu.roll(centre, 1, 1)),
+                jnp.where(last_lane, edge, pltpu.roll(centre, cz - 1, 1)),
+            )
             flow = 2.0 * forc[comp, i]
             for n in range(6):
                 flow = flow + sides[n] * near[n]
@@ -485,7 +492,7 @@
     lax.fori_loop(0, cx, early_one, 0, unroll=UNROLL)
     for wait in waits:
         wait()
-    merged1 = merged_z(1)
+    halos1 = halos_z(1)
 
     for side, i, face, halo_plane in ((0, 0, 0, 0), (1, cx - 1, 1, cx + 1)):
         halo = visc_x[side]
@@ -505,7 +512,7 @@
                 early[comp, i, at : at + 1, :] = early[comp, i, at : at + 1, :] + halo * near
 
     def edges_one(i):
-        return [edge_of(merged1, i)] + [edge_of(merged0, comp * cx + i) for comp in range(3)]
+        return [edge_at(halos1, i, i)]
 
     def values_one(i, edges):
         halo = jnp.where(end_lane, edges[0], 0.0)
@@ -515,7 +522,7 @@
         weight[i] = scale
         z_faces[i] = jnp.where(end_lane, visc[i + 1, rows, :] + halo, 0.0)
         for comp in range(3):
-            flow = early[comp, i] + halo * edges[1 + comp]
+            flow = early[comp, i] + halo * edge0[comp, i]
             value = (1.0 - RELAXATION) * v0[comp, i + 1, rows, :] + scale * flow
             v1[comp, i + 1, rows, :] = value
             keep_end(2, comp, i, value)
@@ -612,11 +619,11 @@
     lax.fori_loop(0, cx, early_two, 0, unroll=UNROLL)
     for wait in waits:
         wait()
-    merged2 = merged_z(2)
+    halos2 = halos_z(2)
     late_planes(2, True)
 
     def edges_two(i):
-        return [edge_of(merged2, comp * cx + i) for comp in range(3)]
+        return [edge_at(halos2, i, comp * cx + i) for comp in range(3)]
 
     def values_two(i, edges):
         factor = z_scaled[i]
@@ -667,12 +674,12 @@
     lax.fori_loop(0, cx, early_misfit, 0, unroll=UNROLL)
     for wait in waits:
         wait()
-    merged3 = merged_z(3)
+    halos3 = halos_z(3)
     late_planes(3, False)
     squares = []
 
     def edges_three(i):
-        return [edge_of(merged3, comp * cx + i) for comp in range(3)]
+        return [edge_of(halos3[1], comp * cx + i) for comp in range(3)]
 
     def values_three(i, edges):
         total = None
@@ -728,17 +735,18 @@
     if not one_stage:
         gather(sums_z, iz, whole, line_peers, line_sem).wait()
         whole = total_of(sums_z)
-    whole = jnp.sum(whole, axis=1, keepdims=True)
-    cells_all = float(3 * cx * nx * cy * ny * cz * nz)
-    rms_ref[...] = jnp.sqrt(whole / cells_all)
-
-
-def writer(*refs):
-    copies = [
-        pltpu.make_async_copy(refs[n], refs[7 + n], refs[14].at[n]) for n in (0, 5, 1, 2, 3, 4, 6)
-    ]
-    for copy in copies:
+    rms_ref[...] = jnp.broadcast_to(whole, rms_ref.shape)
+
+
+def writer(cells_all, *refs):
+    rms, sems = refs[14], refs[15]
+    copies = [pltpu.make_async_copy(refs[n], refs[7 + n], sems.at[n]) for n in (0, 5, 1, 2, 3, 4)]
+    copies.append(pltpu.make_async_copy(rms, refs[13], sems.at[6]))
+    for copy in copies[:6]:
         copy.start()
+    whole = jnp.sum(refs[6][0:1, :], axis=1, keepdims=True)
+    rms[...] = jnp.sqrt(whole / cells_all)
+    copies[6].start()
     for copy in copies:
         copy.wait()
 
@@ -769,7 +777,7 @@
             jax.ShapeDtypeStruct((cx // 4, cy // 4, cz // 4), f32),
             jax.ShapeDtypeStruct((cx // 8, cy // 8, cz // 8), f32),
             jax.ShapeDtypeStruct(velocity.shape, f32),
-            jax.ShapeDtypeStruct((1, 1), f32),
+            jax.ShapeDtypeStruct((8, cz), f32),
         ),
         in_specs=[hbm] * 6,
         out_specs=(vmem,) * 7,
@@ -786,6 +794,7 @@
             v((6, cx, cy, cz), f32),
             v((cx, cy, cz), f32),
             v((cx, cy, cz), f32),
+            v((3, cx, cy, cz), f32),
             v((3, cx, cy, cz), f32),
             v((cx, cy, cz), f32),
             v((cx, cy, cz), f32),
@@ -827,11 +836,12 @@
         ),
     )(*(pltpu.with_memory_space_constraint(a, pltpu.HBM) for a in operands))
     outs = pl.pallas_call(
-        writer,
-        out_shape=tuple(jax.ShapeDtypeStruct(out.shape, f32) for out in outs),
+        functools.partial(writer, float(3 * cx * nx * cy * ny * cz * nz)),
+        out_shape=tuple(jax.ShapeDtypeStruct(out.shape, f32) for out in outs[:6])
+        + (jax.ShapeDtypeStruct((1, 1), f32),),
         in_specs=[vmem] * 7,
         out_specs=(hbm,) * 7,
-        scratch_shapes=[dma((7,))],
+        scratch_shapes=[v((1, 1), f32), dma((7,))],
         compiler_params=pltpu.CompilerParams(vmem_limit_bytes=8 * 1024 * 1024),
     )(*outs)
     return outs[:6] + (outs[6].reshape(()),)

time: 27.1 us -> 25.7 us (0.948)
  Pallas kernels: 26.3 us -> 24.9 us
    pallas_call x1, Pallas kernels: 24.4 us -> 23.6 us  [per_device(): pl.pallas_call(functools.partial(kernel, sizes), out_shape=(jax.ShapeDtyp...]
    pallas_call x1, Pallas kernels: 1.93 us -> 1.3 us  [per_device(): pl.pallas_call(functools.partial(writer, float(3 * cx * nx * cy * ny * cz...]
where the time goes in v5:
time: 25.7 us; the launch traced here: 25.5 us
  Pallas kernels  24.9 us (97%)
  between operations  0.64 us (2%)
    pallas_call x1, Pallas kernels, per_device(): pl.pallas_call(functools.partial(kernel, sizes), out_shape=(jax.ShapeDtyp...  23.6 us
    pallas_call x1, Pallas kernels, per_device(): pl.pallas_call(functools.partial(writer, float(3 * cx * nx * cy * ny * cz...  1.3 us

profile of v5, /device:TPU:0, one launch (start us, length us, event | category | flops | bytes accessed | tf_op | source)
XLA Modules:
  0.0 25.5 jit_solution(13898672367565912681)
XLA Ops:
  0.6 23.6 %shard_map.117 = (f32[3,16,32,128]{3,2,1,0:T(8,128)S(1)}, f32[16,32,128]{2,1,0:T(8,128)S(1)}, f32[8,16,64]{2,1,0:T(8,128)S(1)}, f32[4,8,32]{2,1,0:T(8,128)S(1)},...) custom-call(f32[3,16,32,128]{3,2,1,0:T(8,128)} %vel_hbm.1, ...), custom_call_target="tpu_custom_call" | custom-call | tf_op jit(solution)/shard_map/pallas_call | solution.py:771
  24.2 1.3 %shard_map.118 = (f32[3,16,32,128]{3,2,1,0:T(8,128)}, f32[16,32,128]{2,1,0:T(8,128)}, f32[8,16,64]{2,1,0:T(8,128)}, f32[4,8,32]{2,1,0:T(8,128)}, f32[2,4,16]{2,1...) custom-call(f32[3,16,32,128]{3,2,1,0:T(8,128)S(1)} %get-tuple-element.21.refs_0_, ...), custom_call_target="tpu_custom_call" | custom-call | tf_op jit(solution)/shard_map/pallas_call | solution.py:838

commit v6 on v5

--- a/solution.py
+++ b/solution.py
@@ -215,7 +215,8 @@
 
     lane = lax.broadcasted_iota(jnp.int32, (cy, cz), 1)
     odd_lane = lax.rem(lane, 2) == 1
-    lane_pair = (lane - 1) // 2
+    lane_pair = lax.rem(lane + (cz - 1), cz) // 2
+    own_pair = lane // 2
     first_lane = lane == 0
     last_lane = lane == cz - 1
     end_lane = first_lane | last_lane
@@ -245,16 +246,25 @@
     def send_x(r, last, low, first, high):
         return exchange(3 * r, 0, last, low, first, high)
 
+    def send_y(r):
+        held = pl.ds(0, 1 if r == 1 else 3)
+        return exchange(
+            3 * r + 1, 1,
+            y_send.at[r, 0, held], y_recv.at[r, 0, held],
+            y_send.at[r, 1, held], y_recv.at[r, 1, held],
+        )
+
+    def send_z(r):
+        height = pl.ds(0, visc_rows if r == 1 else cy)
+        return exchange(
+            3 * r + 2, 2,
+            z_send.at[r, height], z_recv.at[r, 0, height],
+            z_send.at[r, height], z_recv.at[r, 1, height],
+        )
+
     def send_yz(r):
-        held = pl.ds(0, 1 if r == 1 else 3)
-        return [
-            exchange(
-                3 * r + 1, 1,
-                y_send.at[r, 0, held], y_recv.at[r, 0, held],
-                y_send.at[r, 1, held], y_recv.at[r, 1, held],
-            ),
-            exchange(3 * r + 2, 2, z_send.at[r], z_recv.at[r, 0], z_send.at[r], z_recv.at[r, 1]),
-        ]
+        sent_z = send_z(r)
+        return [send_y(r), sent_z]
 
     def pack(r, comp, i, value, packed):
         y_send[r, 0, comp, pl.ds(i, 1), :] = value[cy - 1 : cy, :]
@@ -272,9 +282,14 @@
 
         lax.fori_loop(0, cx, body, 0)
 
-    def halos_z(r):
-        low, high = z_recv[r, 0], z_recv[r, 1]
-        return jnp.where(odd_lane, low, high), jnp.where(odd_lane, low, pltpu.roll(high, cz - 2, 1))
+    visc_rows = 8 if 2 * cx * (cy // 8) <= cz else cy
+
+    def halos_z(r, height):
+        low, high = z_recv[r, 0, :height], z_recv[r, 1, :height]
+        odd = odd_lane[:height]
+        if r == 3:
+            return None, jnp.where(odd, pltpu.roll(low, 1, 1), pltpu.roll(high, cz - 1, 1))
+        return jnp.where(odd, low, high), jnp.where(odd, low, pltpu.roll(high, cz - 2, 1))
 
     for copy in ends_in:
         copy.wait()
@@ -341,15 +356,18 @@
         return carry
 
     lax.fori_loop(0, cx, early_strain, 0, unroll=UNROLL)
-    for wait in waits:
+    wait_x, *others = waits
+    for wait in others:
         wait()
-    halos0 = halos_z(0)
-    merged0 = halos0[1]
-    signed0 = [jnp.where(odd_lane, -halo, halo) for halo in halos0]
-    for comp in range(3):
-        n = along_x[comp]
-        faces[n, 0] = faces[n, 0] - x_recv[0, 0, comp]
-        faces[n, cx - 1] = faces[n, cx - 1] + x_recv[0, 1, comp]
+    merged0 = halos_z(0, cy)[1]
+    signed0 = jnp.where(odd_lane, -merged0, merged0)
+
+    def gate_strain():
+        wait_x()
+        for comp in range(3):
+            n = along_x[comp]
+            faces[n, 0] = faces[n, 0] - x_recv[0, 0, comp]
+            faces[n, cx - 1] = faces[n, cx - 1] + x_recv[0, 1, comp]
 
     def late_strain(i):
         for comp in range(3):
@@ -357,13 +375,16 @@
             faces[n, i, 0:1, :] = faces[n, i, 0:1, :] - y_recv[0, 0, comp, pl.ds(i, 1), :]
             faces[n, i, cy - 1 : cy, :] = faces[n, i, cy - 1 : cy, :] + y_recv[0, 1, comp, pl.ds(i, 1), :]
 
-    order = [0, cx - 1] + list(range(1, cx - 1))
-
-    def shell_pass(fix, edge, value_of, r, send_ends, stages):
+    inner, outer = list(range(1, cx - 1)), [0, cx - 1]
+
+    def shell_pass(order, gate, fix, edge, value_of, r, send_ends, stages):
         ahead, hold, behind = stages
-        packed = nothing
+        height, parts = (visc_rows, cy // visc_rows) if r == 1 else (cy, 1)
+        pairs = lane_pair[:height]
+        packed = nothing[:height]
         edges, values, rolled = {}, {}, {}
         sent = None
+        ends_at = [n for n, i in enumerate(order) if i in outer]
         for t in range(cx + ahead + hold + behind):
             if t < cx:
                 edges[t] = edge(order[t])
@@ -371,37 +392,48 @@
             n = t - ahead
             if 0 <= n < cx:
                 i = order[n]
+                if n == ends_at[0]:
+                    gate()
                 values[n] = []
                 for comp, value in enumerate(value_of(i, edges.pop(n))):
                     if r is not None:
                         y_send[r, 0, comp, pl.ds(i, 1), :] = value[cy - 1 : cy, :]
                         y_send[r, 1, comp, pl.ds(i, 1), :] = value[0:1, :]
-                        values[n].append((comp * cx + i, value))
-                if n == 1 and send_ends is not None:
+                        for part in range(parts if r != 3 else 0):
+                            piece = value[part * height : (part + 1) * height, :]
+                            values[n].append(((comp + part) * cx + i, piece))
+                if n == ends_at[1] and send_ends is not None:
                     sent = send_ends()
             n = t - ahead - hold
             if 0 <= n < cx:
-                rolled[n] = [(place, pltpu.roll(value, 2 * place + 2, 1)) for place, value in values.pop(n)]
+                rolled[n] = [(place, turn(value, 2 * place + 2)) for place, value in values.pop(n)]
             n = t - ahead - hold - behind
             if 0 <= n < cx:
                 for place, value in rolled.pop(n):
-                    packed = jnp.where(lane_pair == place, value, packed)
-        if r is None:
-            return None
-        z_send[r] = packed
+                    packed = jnp.where(pairs == place, value, packed)
+        if r is None or r == 3:
+            return sent
+        z_send[r, pl.ds(0, height)] = packed
         return [sent] + send_yz(r)
 
+    def turn(value, amount):
+        return pltpu.roll(value, amount % cz, 1)
+
     def edge_of(merged, place):
-        return pltpu.roll(merged, cz - 1 - 2 * place, 1)
-
-    def edge_at(halos, i, place):
+        return turn(merged, cz - 1 - 2 * place)
+
+    def edge_visc(halos, i):
         mixed, merged = halos
-        if i in (0, cx - 1):
-            return jnp.where(first_lane, edge_of(mixed, place), edge_of(mixed, place + 1))
-        return edge_of(merged, place)
+        places = [part * cx + i for part in range(cy // visc_rows)]
+        if i in outer:
+            first = first_lane[:visc_rows]
+            found = [jnp.where(first, edge_of(mixed, p), edge_of(mixed, p + 1)) for p in places]
+        else:
+            found = [edge_of(merged, p) for p in places]
+        return jnp.concatenate(found, axis=0) if len(found) > 1 else found[0]
 
     def edges_visc(i):
-        return [edge_at(signed0, i, comp * cx + i) for comp in range(3)]
+        return [edge_of(signed0, comp * cx + i) for comp in range(3)]
 
     def values_visc(i, edges):
         strain = [faces[n, i] for n in range(6)]
@@ -421,7 +453,7 @@
     def send_visc():
         return send_x(1, visc.at[cx, rows, :], visc_x.at[0], visc.at[1, rows, :], visc_x.at[1])
 
-    waits = shell_pass(late_strain, edges_visc, values_visc, 1, send_visc, STAGES_VISC)
+    waits = shell_pass(inner + outer, gate_strain, late_strain, edges_visc, values_visc, 1, send_visc, STAGES_VISC)
     for comp in range(3):
         v0[comp, 0, rows, :] = x_recv[0, 0, comp]
         v0[comp, cx + 1, rows, :] = x_recv[0, 1, comp]
@@ -492,7 +524,7 @@
     lax.fori_loop(0, cx, early_one, 0, unroll=UNROLL)
     for wait in waits:
         wait()
-    halos1 = halos_z(1)
+    halos1 = halos_z(1, visc_rows)
 
     for side, i, face, halo_plane in ((0, 0, 0, 0), (1, cx - 1, 1, cx + 1)):
         halo = visc_x[side]
@@ -512,7 +544,7 @@
                 early[comp, i, at : at + 1, :] = early[comp, i, at : at + 1, :] + halo * near
 
     def edges_one(i):
-        return [edge_at(halos1, i, i)]
+        return [edge_visc(halos1, i)]
 
     def values_one(i, edges):
         halo = jnp.where(end_lane, edges[0], 0.0)
@@ -538,7 +570,7 @@
         if i == 0:
             x_send[r - 1, 1, comp] = value
 
-    waits = shell_pass(late_one, edges_one, values_one, 2, send_ends(2), STAGES)
+    waits = shell_pass(outer + inner, lambda: None, late_one, edges_one, values_one, 2, send_ends(2), STAGES)
 
     wait_gx()
     low_y, high_y = flag(has_down[1]), flag(has_up[1])
@@ -596,13 +628,17 @@
             early[comp, i] = (1.0 - RELAXATION) * centre + weight[i] * flow
         return carry
 
-    def late_planes(r, scaled):
-        for side, i, face in ((0, 0, 0), (1, cx - 1, 1)):
-            factor = faces[face, i]
-            if scaled:
-                factor = factor * weight[i]
-            for comp in range(3):
-                early[comp, i] = early[comp, i] + factor * x_recv[r - 1, side, comp]
+    def gate(r, scaled, wait_x):
+        def late_planes():
+            wait_x()
+            for side, i, face in ((0, 0, 0), (1, cx - 1, 1)):
+                factor = faces[face, i]
+                if scaled:
+                    factor = factor * weight[i]
+                for comp in range(3):
+                    early[comp, i] = early[comp, i] + factor * x_recv[r - 1, side, comp]
+
+        return late_planes
 
     def late_rows(r, scaled):
         def fix(i):
@@ -617,13 +653,33 @@
         return fix
 
     lax.fori_loop(0, cx, early_two, 0, unroll=UNROLL)
-    for wait in waits:
-        wait()
-    halos2 = halos_z(2)
-    late_planes(2, True)
+    wait_x, wait_y, wait_z = waits
+
+    def pack_own(packed, value, place):
+        return jnp.where(own_pair == place, turn(value, 2 * place + 1), packed)
+
+    z_weight = nothing
+    for i in range(cx):
+        for comp in range(3):
+            z_weight = pack_own(z_weight, z_scaled[i], comp * cx + i)
+    wait_y()
+    packed = nothing
+    for i in inner:
+        late_rows(2, True)(i)
+        for comp in range(3):
+            packed = pack_own(packed, early[comp, i], comp * cx + i)
+    gate(2, True, wait_x)()
+    for i in outer:
+        late_rows(2, True)(i)
+        for comp in range(3):
+            packed = pack_own(packed, early[comp, i], comp * cx + i)
+    wait_z()
+    merged2 = halos_z(2, cy)[1]
+    z_send[3] = packed + z_weight * merged2
+    sent_z = send_z(3)
 
     def edges_two(i):
-        return [edge_at(halos2, i, comp * cx + i) for comp in range(3)]
+        return [edge_of(merged2, comp * cx + i) for comp in range(3)]
 
     def values_two(i, edges):
         factor = z_scaled[i]
@@ -633,7 +689,8 @@
             keep_end(3, comp, i, value)
             yield value
 
-    waits = shell_pass(late_rows(2, True), edges_two, values_two, 3, send_ends(3), STAGES)
+    sent_x = shell_pass(outer + inner, lambda: None, lambda i: None, edges_two, values_two, 3, send_ends(3), STAGES)
+    waits = [sent_x, send_y(3), sent_z]
 
     wait_gy()
     for buf, k, count, row in ghost_rows:
@@ -672,14 +729,14 @@
         for peer in z_line:
             pl.semaphore_signal(hello_sem, inc=1, device_id=peer, device_id_type=MESH)
     lax.fori_loop(0, cx, early_misfit, 0, unroll=UNROLL)
-    for wait in waits:
+    wait_x, *others = waits
+    for wait in others:
         wait()
-    halos3 = halos_z(3)
-    late_planes(3, False)
+    merged3 = halos_z(3, cy)[1]
     squares = []
 
     def edges_three(i):
-        return [edge_of(halos3[1], comp * cx + i) for comp in range(3)]
+        return [edge_of(merged3, comp * cx + i) for comp in range(3)]
 
     def values_three(i, edges):
         total = None
@@ -690,7 +747,7 @@
             yield value
         squares.append(total if not squares else squares[-1] + total)
 
-    shell_pass(late_rows(3, False), edges_three, values_three, None, None, STAGES)
+    shell_pass(inner + outer, gate(3, False, wait_x), late_rows(3, False), edges_three, values_three, None, None, STAGES)
     part = jnp.sum(squares[-1], axis=0, keepdims=True)
 
     def gather(slots, mine, value, peers, sems):

time: 25.7 us -> 25.3 us (0.984)
  Pallas kernels: 24.9 us -> 24.5 us
    pallas_call x1, Pallas kernels: 23.6 us -> 23.2 us  [per_device(): pl.pallas_call(functools.partial(kernel, sizes), out_shape=(jax.ShapeDtyp...]
where the time goes in v6:
time: 25.3 us; the launch traced here: 25.2 us
  Pallas kernels  24.5 us (97%)
  between operations  0.64 us (3%)
    pallas_call x1, Pallas kernels, per_device(): pl.pallas_call(functools.partial(kernel, sizes), out_shape=(jax.ShapeDtyp...  23.2 us
    pallas_call x1, Pallas kernels, per_device(): pl.pallas_call(functools.partial(writer, float(3 * cx * nx * cy * ny * cz...  1.3 us

profile of v6, /device:TPU:0, one launch (start us, length us, event | category | flops | bytes accessed | tf_op | source)
XLA Modules:
  0.0 25.2 jit_solution(14115638390138167314)
XLA Ops:
  0.6 23.2 %shard_map.117 = (f32[3,16,32,128]{3,2,1,0:T(8,128)S(1)}, f32[16,32,128]{2,1,0:T(8,128)S(1)}, f32[8,16,64]{2,1,0:T(8,128)S(1)}, f32[4,8,32]{2,1,0:T(8,128)S(1)},...) custom-call(f32[3,16,32,128]{3,2,1,0:T(8,128)} %vel_hbm.1, ...), custom_call_target="tpu_custom_call" | custom-call | tf_op jit(solution)/shard_map/pallas_call | solution.py:828
  23.9 1.3 %shard_map.118 = (f32[3,16,32,128]{3,2,1,0:T(8,128)}, f32[16,32,128]{2,1,0:T(8,128)}, f32[8,16,64]{2,1,0:T(8,128)}, f32[4,8,32]{2,1,0:T(8,128)}, f32[2,4,16]{2,1...) custom-call(f32[3,16,32,128]{3,2,1,0:T(8,128)S(1)} %get-tuple-element.21.refs_0_, ...), custom_call_target="tpu_custom_call" | custom-call | tf_op jit(solution)/shard_map/pallas_call | solution.py:895

commit v7 on v6

--- a/solution.py
+++ b/solution.py
@@ -132,7 +132,7 @@
     phase_in = pltpu.make_async_copy(phase_hbm, phase_ref, local_sem.at[7])
     pref_in = pltpu.make_async_copy(pref_hbm, pref_ref, local_sem.at[8])
     yield_in = pltpu.make_async_copy(yield_hbm, yield_ref, local_sem.at[9])
-    for copy in ends_in + vel_in:
+    for copy in vel_in + ends_in:
         copy.start()
 
     barrier = pltpu.get_barrier_semaphore()
@@ -528,7 +528,6 @@
 
     for side, i, face, halo_plane in ((0, 0, 0, 0), (1, cx - 1, 1, cx + 1)):
         halo = visc_x[side]
-        faces[face, i] = faces[face, i] + halo
         diag[i] = diag[i] + halo
         for comp in range(3):
             early[comp, i] = early[comp, i] + halo * v0[comp, halo_plane, rows, :]
@@ -537,7 +536,6 @@
         ends = ((0, 2, 0, PAD - 1), (1, 3, cy - 1, PAD + cy))
         for side, face, at, row in ends:
             halo = y_recv[1, side, 0, pl.ds(i, 1), :]
-            faces[face, i, at : at + 1, :] = faces[face, i, at : at + 1, :] + halo
             diag[i, at : at + 1, :] = diag[i, at : at + 1, :] + halo
             for comp in range(3):
                 near = v0[comp, i + 1, row : row + 1, :]
@@ -621,7 +619,13 @@
             flow = flow + faces[n, i] * near[n]
         return centre, flow
 
+    for side, i, face in ((0, 0, 0), (1, cx - 1, 1)):
+        faces[face, i] = faces[face, i] + visc_x[side]
+
     def early_two(i, carry):
+        for side, face, at in ((0, 2, 0), (1, 3, cy - 1)):
+            halo = y_recv[1, side, 0, pl.ds(i, 1), :]
+            faces[face, i, at : at + 1, :] = faces[face, i, at : at + 1, :] + halo
         z_scaled[i] = weight[i] * z_faces[i]
         for comp in range(3):
             centre, flow = flow_inner(v1, comp, i)

time: 25.3 us -> 25.3 us (level)
  no operation moved by 1% of the time
where the time goes in v7:
time: 25.3 us; the launch traced here: 25.1 us
  Pallas kernels  24.5 us (97%)
  between operations  0.64 us (3%)
    pallas_call x1, Pallas kernels, per_device(): pl.pallas_call(functools.partial(kernel, sizes), out_shape=(jax.ShapeDtyp...  23.2 us
    pallas_call x1, Pallas kernels, per_device(): pl.pallas_call(functools.partial(writer, float(3 * cx * nx * cy * ny * cz...  1.3 us

profile of v7, /device:TPU:0, one launch (start us, length us, event | category | flops | bytes accessed | tf_op | source)
XLA Modules:
  0.0 25.1 jit_solution(1811871205044949036)
XLA Ops:
  0.6 23.2 %shard_map.117 = (f32[3,16,32,128]{3,2,1,0:T(8,128)S(1)}, f32[16,32,128]{2,1,0:T(8,128)S(1)}, f32[8,16,64]{2,1,0:T(8,128)S(1)}, f32[4,8,32]{2,1,0:T(8,128)S(1)},...) custom-call(f32[3,16,32,128]{3,2,1,0:T(8,128)} %vel_hbm.1, ...), custom_call_target="tpu_custom_call" | custom-call | tf_op jit(solution)/shard_map/pallas_call | solution.py:832
  23.8 1.3 %shard_map.118 = (f32[3,16,32,128]{3,2,1,0:T(8,128)}, f32[16,32,128]{2,1,0:T(8,128)}, f32[8,16,64]{2,1,0:T(8,128)}, f32[4,8,32]{2,1,0:T(8,128)}, f32[2,4,16]{2,1...) custom-call(f32[3,16,32,128]{3,2,1,0:T(8,128)S(1)} %get-tuple-element.21.refs_0_, ...), custom_call_target="tpu_custom_call" | custom-call | tf_op jit(solution)/shard_map/pallas_call | solution.py:899
